TPU v7x, 256 devices: a whole 4x4x8 slice. The times are simulated.
256 devices in a mesh: seq: 32 (over y, z_lo, x), exp: 8 (over z_hi, core).
Axes of the slice: x: 4, y: 4, z: 8 (z_hi: 4, z_lo: 2; z = z_hi * 2 + z_lo), core: 2. Of those that a mesh axis runs over, the one named last changes fastest.
Arguments:
- query_input: bfloat16 [4096, 2048], P('seq', 'exp'), may hold values from -4.5 to 4.5
- key_input: bfloat16 [4096, 2048], P('seq', 'exp'), may hold values from -4.5 to 4.5
- value_input: bfloat16 [4096, 2048], P('seq', 'exp'), may hold values from -6 to 6
- segment_ids: int32 [4096], P('seq'), may hold values from 0 to 15, never falling along the last dimension, each value on 1 to 512 neighbouring positions
- residual_in: bfloat16 [4096, 4096], P('seq', 'exp'), may hold values from -13.5 to 13.5
- out_weight: bfloat16 [2048, 4096], P('exp'), may hold values from -0.1875 to 0.1875
- norm_gain: float32 [4096], P('exp'), may hold values from 0.1 to 1.9
- router: bfloat16 [4096, 32], P(None, 'seq'), may hold values from -0.1875 to 0.1875
- modality: int32 [4096], P('seq'), may hold values from 0 to 1
- expert_in: int32 [4096], P('seq'), may hold values from 0 to 15, as said below
- gate_weight: bfloat16 [32, 4096, 2816], P('seq', None, 'exp'), may hold values from -0.09375 to 0.09375
- up_weight: bfloat16 [32, 4096, 2816], P('seq', None, 'exp'), may hold values from -0.09375 to 0.09375
- down_weight: bfloat16 [32, 2816, 4096], P('seq', 'exp'), may hold values from -0.15625 to 0.15625
Outputs:
- layer_out: bfloat16 [4096, 4096], P('seq', 'exp')
Inputs may be any that keep to these rules, and one draw needn't show every extreme that they name: `segment_ids`: document numbers never fall along the sequence, and a document holds at most an eighth of the 4096 tokens. `expert_in`: within each aligned block of 128 tokens no expert (modality and number together) is chosen by more than 7 tokens, and in every block some expert is chosen by exactly 7.
All inputs are finite; a program needn't handle non-finite values.
Results may differ from a plain program's by a relative error of at most 0.0095.
Values may be sent and summed in bfloat16 or wider, within the bound.
A program may use at most 64 MiB of HBM per device.

v0:
```python
import jax
import jax.numpy as jnp
from jax import lax
from jax.sharding import Mesh
from jax.sharding import PartitionSpec as P

D = 4096
HEAD_DIM = 128
EXPERTS = 32
MODAL_EXPERTS = 16
CAPACITY = 7
EXP = ("exp_0", "exp_1")


NEGATIVE = -1e30
EPSILON = 1e-05


def passed_along(value, axis, steps):
    count = lax.axis_size(axis)
    leading, last = (max(0, -steps), min(count, count - steps))
    return lax.ppermute(value, axis, [(source, source + steps) for source in range(leading, last)])


def split_up(array, dim, length):
    lengths = array.shape
    tiles = array.reshape(*lengths[:dim], length, lengths[dim] // length, *lengths[dim + 1 :])
    return jnp.moveaxis(tiles, dim, 0)


def sent_and_summed(array, axis, dim):
    length = lax.axis_size(axis)
    tiles = lax.all_to_all(split_up(array, dim, length), axis, 0, 0, tiled=True)
    return jnp.sum(tiles.astype(jnp.float32), axis=0)


def copy_for_each(array, axis):
    copies = jnp.broadcast_to(array, (lax.axis_size(axis), *array.shape))
    return lax.all_to_all(copies, axis, split_axis=0, concat_axis=0, tiled=True)


def over_copies(array, axis):
    everything = copy_for_each(array, axis)
    return jnp.sum(everything, axis=0)


def joined_along(tiles, dim):
    tiles = jnp.moveaxis(tiles, 0, dim)
    lengths = tiles.shape
    return tiles.reshape(*lengths[:dim], lengths[dim] * lengths[dim + 1], *lengths[dim + 2 :])


def stacked_from(array, axes, turns):
    tiles = array
    for k in turns:
        tiles = lax.all_gather(tiles, axes[k])
    done = turns[::-1]
    back = [done.index(k) for k in range(len(axes))]
    tiles = tiles.transpose(*back, *range(len(axes), tiles.ndim))
    return tiles.reshape(-1, *array.shape)


def gather_axes(array, axes, turns, dim):
    return joined_along(stacked_from(array, axes, turns), dim)


def absorb(carry_state, query_heads, key_block, value_block, allowed):
    running_max, denominators, numerators = carry_state
    scores = jnp.einsum(
        "qhd,khd->hqk", query_heads, key_block, preferred_element_type=jnp.float32
    ) * HEAD_DIM ** (-0.5)
    masked = jnp.where(allowed[None], scores, NEGATIVE)
    new_max = jnp.maximum(running_max, jnp.max(masked, axis=2))
    rescale = jnp.exp(running_max - new_max)
    weights = jnp.exp(masked - new_max[:, :, None])
    denominators = denominators * rescale + jnp.sum(weights, axis=2)
    numerators = numerators * rescale[:, :, None] + jnp.einsum(
        "hqk,khd->hqd",
        weights.astype(jnp.bfloat16),
        value_block,
        preferred_element_type=jnp.float32,
    )
    return (new_max, denominators, numerators)


def local(
    query_input,
    key_input,
    value_input,
    segment_ids,
    residual_in,
    out_weight,
    norm_gain,
    router,
    modality,
    expert_in,
    gate_weight,
    up_weight,
    down_weight,
):
    token_count = query_input.shape[0]
    head_count = query_input.shape[1] // HEAD_DIM
    query_heads = query_input.reshape(token_count, head_count, HEAD_DIM)
    key_heads = key_input.reshape(token_count, head_count, HEAD_DIM)
    value_heads = value_input.reshape(token_count, head_count, HEAD_DIM)
    positions = jnp.arange(token_count, dtype=jnp.int32)
    local_mask = (segment_ids[:, None] == segment_ids[None, :]) & (
        positions[None, :] <= positions[:, None]
    )
    empty_state = (
        jnp.full((head_count, token_count), NEGATIVE, jnp.float32),
        jnp.zeros((head_count, token_count), jnp.float32),
        jnp.zeros((head_count, token_count, HEAD_DIM), jnp.float32),
    )
    carry_state = absorb(empty_state, query_heads, key_heads, value_heads, local_mask)
    cycle_index = lax.axis_index("seq")

    def visit(step_number, loop_carry):
        visit_state, key_block, value_block, travel_segments = loop_carry
        key_block, value_block, travel_segments = passed_along(
            (key_block, value_block, travel_segments), "seq", 1
        )
        has_block = cycle_index - step_number - 1 >= 0
        allowed = has_block & (segment_ids[:, None] == travel_segments.astype(jnp.int32)[None, :])
        visit_state = absorb(visit_state, query_heads, key_block, value_block, allowed)
        return (visit_state, key_block, value_block, travel_segments)

    start_carry = (carry_state, key_heads, value_heads, segment_ids.astype(jnp.bfloat16))
    final_carry = lax.fori_loop(0, lax.axis_size("seq") // 8, visit, start_carry)
    running_max, denominators, numerators = final_carry[0]
    attended = (numerators / denominators[:, :, None]).astype(jnp.bfloat16)
    attended = jnp.transpose(attended, (1, 0, 2)).reshape(token_count, head_count * HEAD_DIM)
    projected = jnp.dot(attended, out_weight, preferred_element_type=jnp.float32)
    attention = sent_and_summed(projected.astype(jnp.bfloat16), EXP, 1)
    residual = residual_in.astype(jnp.float32) + attention
    squares = jnp.sum(residual * residual, axis=1)
    square_total = over_copies(squares, EXP)
    normed = (residual * lax.rsqrt(square_total / D + EPSILON)[:, None] * norm_gain).astype(
        jnp.bfloat16
    )
    picked = modality * MODAL_EXPERTS + expert_in
    one_hot = (picked[:, None] == jnp.arange(EXPERTS, dtype=jnp.int32)[None, :]).astype(jnp.int32)
    rank_in_block = jnp.sum(one_hot * (jnp.cumsum(one_hot, axis=0) - 1), axis=1)
    slot_index = picked * CAPACITY + rank_in_block
    outgoing = (
        jnp.zeros((EXPERTS * CAPACITY, normed.shape[1]), jnp.bfloat16).at[slot_index].set(normed)
    )
    sliced = lax.all_to_all(
        outgoing.reshape(EXPERTS, CAPACITY, normed.shape[1]),
        "seq",
        split_axis=0,
        concat_axis=1,
        tiled=True,
    )
    arrived = gather_axes(sliced, EXP, (0, 1), 2)
    gate_sum = jnp.einsum("erd,edf->erf", arrived, gate_weight, preferred_element_type=jnp.float32)
    up_sum = jnp.einsum("erd,edf->erf", arrived, up_weight, preferred_element_type=jnp.float32)
    logits = jnp.einsum("erd,de->er", arrived, router, preferred_element_type=jnp.float32)
    hidden = (jax.nn.silu(gate_sum) * up_sum * jax.nn.sigmoid(logits)[:, :, None]).astype(
        jnp.bfloat16
    )
    partial_value = jnp.einsum(
        "erf,efd->erd", hidden, down_weight, preferred_element_type=jnp.float32
    )
    summed = lax.psum_scatter(
        partial_value.astype(jnp.bfloat16), EXP, scatter_dimension=2, tiled=True
    )
    returned = lax.all_to_all(summed, "seq", split_axis=1, concat_axis=0, tiled=True)
    routed = returned.reshape(EXPERTS * CAPACITY, returned.shape[2])[slot_index]
    return (residual + routed.astype(jnp.float32)).astype(jnp.bfloat16)


def solution(mesh):
    split = Mesh(mesh.devices.reshape(mesh.shape["seq"], 4, 2), ("seq", "exp_0", "exp_1"))
    placed = (
        P("seq", EXP),
        P("seq", EXP),
        P("seq", EXP),
        P("seq"),
        P("seq", EXP),
        P(EXP, None),
        P(EXP),
        P(None, "seq"),
        P("seq"),
        P("seq"),
        P("seq", None, EXP),
        P("seq", None, EXP),
        P("seq", EXP, None),
    )
    return jax.shard_map(
        local, mesh=split, in_specs=placed, out_specs=P("seq", EXP), check_vma=False
    )
```

profile of v0, /device:TPU:1, one launch (start us, length us, event | category | flops | bytes accessed | tf_op | source)
XLA Modules:
  0.0 264.6 jit_solution(9415738646136405745)
XLA Ops:
  11.9 48.1 %while.25 = (s32[]{:T(128)}, f32[2,128]{1,0:T(2,128)S(1)}, f32[2,128]{1,0:T(2,128)S(1)}, f32[2,128,128]{2,1,0:T(8,128)S(1)}, bf16[128,2,128]{2,0,1:T(8,128)(2,1)...) while((s32[]{:T(128)}, f32[2,128]{1,0:T(2,128)S(1)}, ...), condition=%wide.region_5.6_spmd, body=%wide.region_2.5_spmd.sunk | while | flops 17171076 | bytes 1723927 | solution.py:129
  11.9 3.9 %collective-permute-start = (bf16[128]{0:T(256)(128)(2,1)S(1)}, bf16[128]{0:T(256)(128)(2,1)S(1)}, u32[]{:S(2)}, u32[]{:S(2)}) collective-permute-start(bf16[128]{0:T(256)(128)(2,1)S(1)} %get-tuple-element.416), channel_id=1, source_target_pairs={{0,8},{8,16},{16,24},{24,32},{32,40},{40,48},{48,56},{56,64},{64,7... | collective-permute-start | bytes 776 | tf_op jit(solution)/shard_map/while/body/eval_jaxpr/ppermute | solution.py:22
  15.9 3.1 %collective-permute-start.1 = (bf16[128,2,128]{2,0,1:T(8,128)(2,1)S(1)}, bf16[128,2,128]{2,0,1:T(8,128)(2,1)S(1)}, u32[]{:S(2)}, u32[]{:S(2)}) collective-permute-start(bf16[128,2,128]{2,0,1:T(8,128)(2,1)S(1)} %get-tuple-element.414), channel_id=1, source_target_pairs={{0,8},{8,16},{16,24},{24,32},{32,40},{40,48},{48,56},{56,64},{64,7... | collective-permute-start | bytes 196616 | tf_op jit(solution)/shard_map/while/body/eval_jaxpr/ppermute | solution.py:22
  19.0 2.8 %collective-permute-start.2 = (bf16[128,2,128]{2,0,1:T(8,128)(2,1)S(1)}, bf16[128,2,128]{2,0,1:T(8,128)(2,1)S(1)}, u32[]{:S(2)}, u32[]{:S(2)}) collective-permute-start(bf16[128,2,128]{2,0,1:T(8,128)(2,1)S(1)} %get-tuple-element.415), channel_id=1, source_target_pairs={{0,8},{8,16},{16,24},{24,32},{32,40},{40,48},{48,56},{56,64},{64,7... | collective-permute-start | bytes 196616 | tf_op jit(solution)/shard_map/while/body/eval_jaxpr/ppermute | solution.py:22
  23.4 3.7 %collective-permute-start = (bf16[128]{0:T(256)(128)(2,1)S(1)}, bf16[128]{0:T(256)(128)(2,1)S(1)}, u32[]{:S(2)}, u32[]{:S(2)}) collective-permute-start(bf16[128]{0:T(256)(128)(2,1)S(1)} %get-tuple-element.416), channel_id=1, source_target_pairs={{0,8},{8,16},{16,24},{24,32},{32,40},{40,48},{48,56},{56,64},{64,7... | collective-permute-start | bytes 776 | tf_op jit(solution)/shard_map/while/body/eval_jaxpr/ppermute | solution.py:22
  27.1 3.5 %collective-permute-start.1 = (bf16[128,2,128]{2,0,1:T(8,128)(2,1)S(1)}, bf16[128,2,128]{2,0,1:T(8,128)(2,1)S(1)}, u32[]{:S(2)}, u32[]{:S(2)}) collective-permute-start(bf16[128,2,128]{2,0,1:T(8,128)(2,1)S(1)} %get-tuple-element.414), channel_id=1, source_target_pairs={{0,8},{8,16},{16,24},{24,32},{32,40},{40,48},{48,56},{56,64},{64,7... | collective-permute-start | bytes 196616 | tf_op jit(solution)/shard_map/while/body/eval_jaxpr/ppermute | solution.py:22
  30.6 3.1 %collective-permute-start.2 = (bf16[128,2,128]{2,0,1:T(8,128)(2,1)S(1)}, bf16[128,2,128]{2,0,1:T(8,128)(2,1)S(1)}, u32[]{:S(2)}, u32[]{:S(2)}) collective-permute-start(bf16[128,2,128]{2,0,1:T(8,128)(2,1)S(1)} %get-tuple-element.415), channel_id=1, source_target_pairs={{0,8},{8,16},{16,24},{24,32},{32,40},{40,48},{48,56},{56,64},{64,7... | collective-permute-start | bytes 196616 | tf_op jit(solution)/shard_map/while/body/eval_jaxpr/ppermute | solution.py:22
  35.9 4.6 %collective-permute-start = (bf16[128]{0:T(256)(128)(2,1)S(1)}, bf16[128]{0:T(256)(128)(2,1)S(1)}, u32[]{:S(2)}, u32[]{:S(2)}) collective-permute-start(bf16[128]{0:T(256)(128)(2,1)S(1)} %get-tuple-element.416), channel_id=1, source_target_pairs={{0,8},{8,16},{16,24},{24,32},{32,40},{40,48},{48,56},{56,64},{64,7... | collective-permute-start | bytes 776 | tf_op jit(solution)/shard_map/while/body/eval_jaxpr/ppermute | solution.py:22
  40.5 3.7 %collective-permute-start.1 = (bf16[128,2,128]{2,0,1:T(8,128)(2,1)S(1)}, bf16[128,2,128]{2,0,1:T(8,128)(2,1)S(1)}, u32[]{:S(2)}, u32[]{:S(2)}) collective-permute-start(bf16[128,2,128]{2,0,1:T(8,128)(2,1)S(1)} %get-tuple-element.414), channel_id=1, source_target_pairs={{0,8},{8,16},{16,24},{24,32},{32,40},{40,48},{48,56},{56,64},{64,7... | collective-permute-start | bytes 196616 | tf_op jit(solution)/shard_map/while/body/eval_jaxpr/ppermute | solution.py:22
  44.2 1.9 collective-permute-start.2
  47.8 4.0 %collective-permute-start = (bf16[128]{0:T(256)(128)(2,1)S(1)}, bf16[128]{0:T(256)(128)(2,1)S(1)}, u32[]{:S(2)}, u32[]{:S(2)}) collective-permute-start(bf16[128]{0:T(256)(128)(2,1)S(1)} %get-tuple-element.416), channel_id=1, source_target_pairs={{0,8},{8,16},{16,24},{24,32},{32,40},{40,48},{48,56},{56,64},{64,7... | collective-permute-start | bytes 776 | tf_op jit(solution)/shard_map/while/body/eval_jaxpr/ppermute | solution.py:22
  51.8 4.2 %collective-permute-start.1 = (bf16[128,2,128]{2,0,1:T(8,128)(2,1)S(1)}, bf16[128,2,128]{2,0,1:T(8,128)(2,1)S(1)}, u32[]{:S(2)}, u32[]{:S(2)}) collective-permute-start(bf16[128,2,128]{2,0,1:T(8,128)(2,1)S(1)} %get-tuple-element.414), channel_id=1, source_target_pairs={{0,8},{8,16},{16,24},{24,32},{32,40},{40,48},{48,56},{56,64},{64,7... | collective-permute-start | bytes 196616 | tf_op jit(solution)/shard_map/while/body/eval_jaxpr/ppermute | solution.py:22
  56.0 2.5 collective-permute-start.2
  60.2 2.1 convolution_convert_fusion.1
  63.4 15.5 %all-to-all-start = ((bf16[8,128,512]{2,1,0:T(8,128)(2,1)}), bf16[8,128,512]{2,1,0:T(8,128)(2,1)}, u32[]{:S(2)}, u32[]{:S(2)}) async-start(bf16[8,128,512]{2,1,0:T(8,128)(2,1)} %bitcast.76), calls=%async_computation | async-start | bytes 2097152 | tf_op jit(solution)/shard_map/all_to_all | solution.py:33
  79.4 21.1 %all-to-all-done = bf16[8,128,512]{2,1,0:T(8,128)(2,1)} async-done(((bf16[8,128,512]{2,1,0:T(8,128)(2,1)}), bf16[8,128,512]{2,1,0:T(8,128)(2,1)}, u32[]{:S(2)}, u32[]{:S(2)}) %all-to-all-start) | async-done | bytes 1048608 | tf_op jit(solution)/shard_map/all_to_all | solution.py:33
  102.6 11.3 %all-to-all-start.1 = ((f32[8,1,128]{2,1,0:T(1,128)}), f32[8,1,128]{2,1,0:T(1,128)S(1)}, u32[]{:S(2)}, u32[]{:S(2)}) async-start(f32[8,1,128]{2,1,0:T(1,128)} %broadcast_in_dim.92), calls=%async_computation.1 | async-start | bytes 8192 | tf_op jit(solution)/shard_map/all_to_all | solution.py:39
  114.0 6.9 %all-to-all-done.1 = f32[8,1,128]{2,1,0:T(1,128)S(1)} async-done(((f32[8,1,128]{2,1,0:T(1,128)}), f32[8,1,128]{2,1,0:T(1,128)S(1)}, u32[]{:S(2)}, u32[]{:S(2)}) %all-to-all-start.1) | async-done | bytes 4128 | tf_op jit(solution)/shard_map/all_to_all | solution.py:39
  122.9 18.8 %all_to_all.29 = bf16[32,7,512]{2,1,0:T(8,128)(2,1)} all-to-all(bf16[32,7,512]{2,1,0:T(8,128)(2,1)} %reshape.170), channel_id=1, replica_groups=mesh['seq'=32,'exp_0'=4,'exp_1'=2] {'seq'}, dimensions={0} | all-to-all | bytes 458752 | tf_op jit(solution)/shard_map/all_to_all | solution.py:148
  142.7 17.2 %all_gather.13 = bf16[4,1,224,512]{3,2,1,0:T(8,128)(2,1)} all-gather(bf16[1,1,224,512]{3,2,1,0:T(8,128)(2,1)S(1)} %all_gather.12), channel_id=1, replica_groups=mesh['seq'=32,'exp_0'=4,'exp_1'=2] {'exp_0'}, dimensions={0}, use_global_device_ids=true | all-gather | bytes 1146880 | tf_op jit(solution)/shard_map/all_gather | solution.py:56
  160.0 16.6 %all-gather.3.cloned.1.call-done = bf16[8,1,224,512]{3,2,1,0:T(8,128)(2,1)} async-done(((bf16[4,1,224,512]{3,2,1,0:T(8,128)(2,1)}), bf16[8,1,224,512]{3,2,1,0:T(8,128)(2,1)}) %all-gather.3.cloned.1.call-update) | async-done | bytes 1835024 | tf_op jit(solution)/shard_map/all_gather | solution.py:56
  176.6 1.7 copy.91
  178.5 2.2 copy-done.5
  180.8 1.9 fusion.11
  183.3 6.1 %fusion.7 = bf16[1,224,4096]{2,1,0:T(8,128)(2,1)} fusion(bf16[1,352,4096]{2,1,0:T(8,128)(2,1)S(1)} %copy-done, bf16[224,4096]{1,0:T(8,128)(2,1)} %bitcast.72, bf16[1,4096,352]{1,2,0:T(8,128)(2,1)} %param.26, f32[224,352]{1,0:T(8,128)} %fusion.11, f32[224]{0:T(256)S(1)} %add_divide_fusion), kind=kOutput, calls=%fused_computation.16 | convolution fusion | flops 1293315072 | bytes 9753472 | tf_op jit(solution)/shard_map/erf,efd->erd/dot_general | solution.py:162
  189.4 41.8 %reduce-scatter.2.cloned.1.call-done = bf16[1,224,512]{2,1,0:T(8,128)(2,1)} async-done(((bf16[1,224,4096]{2,1,0:T(8,128)(2,1)}), bf16[1,224,512]{2,1,0:T(8,128)(2,1)}) %reduce-scatter.2.cloned.1.call-update) | async-done | bytes 229392 | tf_op jit(solution)/shard_map/reduce_scatter | solution.py:165
  231.2 2.1 copy.108
  233.8 2.9 %reduce.1 = bf16[224,512]{1,0:T(8,128)(2,1)S(1)} reduce(bf16[224,1,512]{2,1,0:T(2,128)(2,1)} %bitcast.78, bf16[]{:T(256)} %broadcast.146), dimensions={1}, to_apply=%bitcast.63.reduce_sub_computation | reduce | bytes 458754
  237.5 7.2 %all-to-all-start.3 = ((bf16[32,2,1792]{2,1,0:T(2,128)(2,1)}), bf16[32,2,1792]{2,1,0:T(2,128)(2,1)S(1)}, u32[]{:S(2)}, u32[]{:S(2)}) async-start(bf16[32,2,1792]{2,1,0:T(2,128)(2,1)} %reshape.202), calls=%async_computation.4 | async-start | bytes 458752 | tf_op jit(solution)/shard_map/all_to_all | solution.py:168
  244.8 7.9 %all-to-all-done.3 = bf16[32,2,1792]{2,1,0:T(2,128)(2,1)S(1)} async-done(((bf16[32,2,1792]{2,1,0:T(2,128)(2,1)}), bf16[32,2,1792]{2,1,0:T(2,128)(2,1)S(1)}, u32[]{:S(2)}, u32[]{:S(2)}) %all-to-all-start.3) | async-done | bytes 229408 | tf_op jit(solution)/shard_map/all_to_all | solution.py:168
  254.7 1.5 gather_fusion
  256.2 1.6 add_convert_fusion
  (112 shorter events, 22.9 us)
Async XLA Ops:
  6.5 176.8 %copy-start = (bf16[1,352,4096]{2,1,0:T(8,128)(2,1)S(1)}, bf16[1,352,4096]{2,1,0:T(8,128)(2,1)}, u32[]{:S(2)}) copy-start(bf16[1,352,4096]{2,1,0:T(8,128)(2,1)} %param.27) | copy-start | bytes 8650756
  11.9 9.9 %collective-permute-start = (bf16[128]{0:T(256)(128)(2,1)S(1)}, bf16[128]{0:T(256)(128)(2,1)S(1)}, u32[]{:S(2)}, u32[]{:S(2)}) collective-permute-start(bf16[128]{0:T(256)(128)(2,1)S(1)} %get-tuple-element.416), channel_id=1, source_target_pairs={{0,8},{8,16},{16,24},{24,32},{32,40},{40,48},{48,56},{56,64},{64,7... | collective-permute-start | bytes 776 | tf_op jit(solution)/shard_map/while/body/eval_jaxpr/ppermute | solution.py:22
  15.9 6.8 %collective-permute-start.1 = (bf16[128,2,128]{2,0,1:T(8,128)(2,1)S(1)}, bf16[128,2,128]{2,0,1:T(8,128)(2,1)S(1)}, u32[]{:S(2)}, u32[]{:S(2)}) collective-permute-start(bf16[128,2,128]{2,0,1:T(8,128)(2,1)S(1)} %get-tuple-element.414), channel_id=1, source_target_pairs={{0,8},{8,16},{16,24},{24,32},{32,40},{40,48},{48,56},{56,64},{64,7... | collective-permute-start | bytes 196616 | tf_op jit(solution)/shard_map/while/body/eval_jaxpr/ppermute | solution.py:22
  19.0 4.1 %collective-permute-start.2 = (bf16[128,2,128]{2,0,1:T(8,128)(2,1)S(1)}, bf16[128,2,128]{2,0,1:T(8,128)(2,1)S(1)}, u32[]{:S(2)}, u32[]{:S(2)}) collective-permute-start(bf16[128,2,128]{2,0,1:T(8,128)(2,1)S(1)} %get-tuple-element.415), channel_id=1, source_target_pairs={{0,8},{8,16},{16,24},{24,32},{32,40},{40,48},{48,56},{56,64},{64,7... | collective-permute-start | bytes 196616 | tf_op jit(solution)/shard_map/while/body/eval_jaxpr/ppermute | solution.py:22
  23.4 10.3 %collective-permute-start = (bf16[128]{0:T(256)(128)(2,1)S(1)}, bf16[128]{0:T(256)(128)(2,1)S(1)}, u32[]{:S(2)}, u32[]{:S(2)}) collective-permute-start(bf16[128]{0:T(256)(128)(2,1)S(1)} %get-tuple-element.416), channel_id=1, source_target_pairs={{0,8},{8,16},{16,24},{24,32},{32,40},{40,48},{48,56},{56,64},{64,7... | collective-permute-start | bytes 776 | tf_op jit(solution)/shard_map/while/body/eval_jaxpr/ppermute | solution.py:22
  27.1 7.4 %collective-permute-start.1 = (bf16[128,2,128]{2,0,1:T(8,128)(2,1)S(1)}, bf16[128,2,128]{2,0,1:T(8,128)(2,1)S(1)}, u32[]{:S(2)}, u32[]{:S(2)}) collective-permute-start(bf16[128,2,128]{2,0,1:T(8,128)(2,1)S(1)} %get-tuple-element.414), channel_id=1, source_target_pairs={{0,8},{8,16},{16,24},{24,32},{32,40},{40,48},{48,56},{56,64},{64,7... | collective-permute-start | bytes 196616 | tf_op jit(solution)/shard_map/while/body/eval_jaxpr/ppermute | solution.py:22
  30.6 5.0 %collective-permute-start.2 = (bf16[128,2,128]{2,0,1:T(8,128)(2,1)S(1)}, bf16[128,2,128]{2,0,1:T(8,128)(2,1)S(1)}, u32[]{:S(2)}, u32[]{:S(2)}) collective-permute-start(bf16[128,2,128]{2,0,1:T(8,128)(2,1)S(1)} %get-tuple-element.415), channel_id=1, source_target_pairs={{0,8},{8,16},{16,24},{24,32},{32,40},{40,48},{48,56},{56,64},{64,7... | collective-permute-start | bytes 196616 | tf_op jit(solution)/shard_map/while/body/eval_jaxpr/ppermute | solution.py:22
  35.9 10.3 %collective-permute-start = (bf16[128]{0:T(256)(128)(2,1)S(1)}, bf16[128]{0:T(256)(128)(2,1)S(1)}, u32[]{:S(2)}, u32[]{:S(2)}) collective-permute-start(bf16[128]{0:T(256)(128)(2,1)S(1)} %get-tuple-element.416), channel_id=1, source_target_pairs={{0,8},{8,16},{16,24},{24,32},{32,40},{40,48},{48,56},{56,64},{64,7... | collective-permute-start | bytes 776 | tf_op jit(solution)/shard_map/while/body/eval_jaxpr/ppermute | solution.py:22
  40.5 6.4 %collective-permute-start.1 = (bf16[128,2,128]{2,0,1:T(8,128)(2,1)S(1)}, bf16[128,2,128]{2,0,1:T(8,128)(2,1)S(1)}, u32[]{:S(2)}, u32[]{:S(2)}) collective-permute-start(bf16[128,2,128]{2,0,1:T(8,128)(2,1)S(1)} %get-tuple-element.414), channel_id=1, source_target_pairs={{0,8},{8,16},{16,24},{24,32},{32,40},{40,48},{48,56},{56,64},{64,7... | collective-permute-start | bytes 196616 | tf_op jit(solution)/shard_map/while/body/eval_jaxpr/ppermute | solution.py:22
  44.2 3.2 %collective-permute-start.2 = (bf16[128,2,128]{2,0,1:T(8,128)(2,1)S(1)}, bf16[128,2,128]{2,0,1:T(8,128)(2,1)S(1)}, u32[]{:S(2)}, u32[]{:S(2)}) collective-permute-start(bf16[128,2,128]{2,0,1:T(8,128)(2,1)S(1)} %get-tuple-element.415), channel_id=1, source_target_pairs={{0,8},{8,16},{16,24},{24,32},{32,40},{40,48},{48,56},{56,64},{64,7... | collective-permute-start | bytes 196616 | tf_op jit(solution)/shard_map/while/body/eval_jaxpr/ppermute | solution.py:22
  47.8 10.7 %collective-permute-start = (bf16[128]{0:T(256)(128)(2,1)S(1)}, bf16[128]{0:T(256)(128)(2,1)S(1)}, u32[]{:S(2)}, u32[]{:S(2)}) collective-permute-start(bf16[128]{0:T(256)(128)(2,1)S(1)} %get-tuple-element.416), channel_id=1, source_target_pairs={{0,8},{8,16},{16,24},{24,32},{32,40},{40,48},{48,56},{56,64},{64,7... | collective-permute-start | bytes 776 | tf_op jit(solution)/shard_map/while/body/eval_jaxpr/ppermute | solution.py:22
  51.8 7.5 %collective-permute-start.1 = (bf16[128,2,128]{2,0,1:T(8,128)(2,1)S(1)}, bf16[128,2,128]{2,0,1:T(8,128)(2,1)S(1)}, u32[]{:S(2)}, u32[]{:S(2)}) collective-permute-start(bf16[128,2,128]{2,0,1:T(8,128)(2,1)S(1)} %get-tuple-element.414), channel_id=1, source_target_pairs={{0,8},{8,16},{16,24},{24,32},{32,40},{40,48},{48,56},{56,64},{64,7... | collective-permute-start | bytes 196616 | tf_op jit(solution)/shard_map/while/body/eval_jaxpr/ppermute | solution.py:22
  56.0 3.8 %collective-permute-start.2 = (bf16[128,2,128]{2,0,1:T(8,128)(2,1)S(1)}, bf16[128,2,128]{2,0,1:T(8,128)(2,1)S(1)}, u32[]{:S(2)}, u32[]{:S(2)}) collective-permute-start(bf16[128,2,128]{2,0,1:T(8,128)(2,1)S(1)} %get-tuple-element.415), channel_id=1, source_target_pairs={{0,8},{8,16},{16,24},{24,32},{32,40},{40,48},{48,56},{56,64},{64,7... | collective-permute-start | bytes 196616 | tf_op jit(solution)/shard_map/while/body/eval_jaxpr/ppermute | solution.py:22
  62.3 16.7 %copy-start.6 = (s32[128]{0:T(128)S(1)}, s32[128]{0:T(128)}, u32[]{:S(2)}) copy-start(s32[128]{0:T(128)} %param.24) | copy-start | bytes 1540
  62.3 16.7 %copy-start.7 = (s32[128]{0:T(128)S(1)}, s32[128]{0:T(128)}, u32[]{:S(2)}) copy-start(s32[128]{0:T(128)} %param.23) | copy-start | bytes 1540
  63.4 38.5 %copy-start.2 = (bf16[128,512]{1,0:T(8,128)(2,1)S(1)}, bf16[128,512]{1,0:T(8,128)(2,1)}, u32[]{:S(2)}) copy-start(bf16[128,512]{1,0:T(8,128)(2,1)} %param.19) | copy-start | bytes 393220
  63.4 57.5 %copy-start.4 = (f32[512]{0:T(512)S(1)}, f32[512]{0:T(512)}, u32[]{:S(2)}) copy-start(f32[512]{0:T(512)} %param.21) | copy-start | bytes 6148
  63.4 37.1 %all-to-all-start = ((bf16[8,128,512]{2,1,0:T(8,128)(2,1)}), bf16[8,128,512]{2,1,0:T(8,128)(2,1)}, u32[]{:S(2)}, u32[]{:S(2)}) async-start(bf16[8,128,512]{2,1,0:T(8,128)(2,1)} %bitcast.76), calls=%async_computation | async-start | bytes 2097152 | tf_op jit(solution)/shard_map/all_to_all | solution.py:33
  102.6 18.3 %all-to-all-start.1 = ((f32[8,1,128]{2,1,0:T(1,128)}), f32[8,1,128]{2,1,0:T(1,128)S(1)}, u32[]{:S(2)}, u32[]{:S(2)}) async-start(f32[8,1,128]{2,1,0:T(1,128)} %broadcast_in_dim.92), calls=%async_computation.1 | async-start | bytes 8192 | tf_op jit(solution)/shard_map/all_to_all | solution.py:39
  114.0 62.6 %all-gather.3.cloned.1.call-start = ((), (), s32[]{:S(2)}) async-start(), calls=%async_computation.6 | async-start | bytes 2752512 | tf_op jit(solution)/shard_map/all_gather | solution.py:56
  159.9 71.3 %reduce-scatter.2.cloned.1.call-start = ((), (), s32[]{:S(2)}) async-start(), calls=%async_computation.5 | async-start | bytes 2064384 | tf_op jit(solution)/shard_map/reduce_scatter | solution.py:165
  178.3 2.5 copy-start.5
  178.5 4.2 %copy-start.1 = (bf16[28,8,8,512]{3,1,2,0:T(8,128)(2,1)}, bf16[28,8,8,512]{3,1,2,0:T(8,128)(2,1)S(1)}, u32[]{:S(2)}) copy-start(bf16[28,8,8,512]{3,1,2,0:T(8,128)(2,1)S(1)} %copy.101) | copy-start | bytes 5505028
  180.8 1.9 copy-start.3
  237.5 15.2 %all-to-all-start.3 = ((bf16[32,2,1792]{2,1,0:T(2,128)(2,1)}), bf16[32,2,1792]{2,1,0:T(2,128)(2,1)S(1)}, u32[]{:S(2)}, u32[]{:S(2)}) async-start(bf16[32,2,1792]{2,1,0:T(2,128)(2,1)} %reshape.202), calls=%async_computation.4 | async-start | bytes 458752 | tf_op jit(solution)/shard_map/all_to_all | solution.py:168
Sparse Core Ops, SparseCore 0:
  160.1 16.4 all-gather.2
  189.5 41.6 reduce-scatter.1
where the time goes:
time: 267 us; the launch traced here: 265 us
  waiting for transfers between devices  95.8 us (36%)
  starting transfers between devices  75.3 us (28%)
  blocking collectives  36 us (13%)
  local copies, waits for them, and re-layouts  18 us (7%)
  between operations  13.6 us (5%)
  matrix products  12.9 us (5%)
  other arithmetic  12.6 us (5%)
    reduce_scatter x1, waiting for transfers between devices, local(): lax.psum_scatter(partial_value.astype(jnp.bfloat16), EXP, scatter_dimensi...  41.8 us
    ppermute x12, starting transfers between devices, passed_along(): lax.ppermute(value, axis, [(source, source + steps) for source in range(l...  41.1 us
    all_to_all x1, waiting for transfers between devices, sent_and_summed(): tiles = lax.all_to_all(split_up(array, dim, length), axis, 0, 0, tiled=True)  21.1 us
    all_to_all x1, blocking collectives, local(): lax.all_to_all(outgoing.reshape(EXPERTS, CAPACITY, normed.shape[1]), 'seq...  18.8 us
    all_gather x1, blocking collectives, stacked_from(): tiles = lax.all_gather(tiles, axes[k])  17.2 us
    all_gather x1, waiting for transfers between devices, stacked_from(): tiles = lax.all_gather(tiles, axes[k])  16.6 us
    all_to_all x1, starting transfers between devices, sent_and_summed(): tiles = lax.all_to_all(split_up(array, dim, length), axis, 0, 0, tiled=True)  15.5 us
    all_to_all x1, starting transfers between devices, copy_for_each(): return lax.all_to_all(copies, axis, split_axis=0, concat_axis=0, tiled=True)  11.3 us
  transfers between devices with their start and end apart: 17, of which 9 were waited for; matrix products, arithmetic and copies ran while one was open for 2% of the time, Pallas kernels for 0%

commit v1 on v0

v1 whole, which is shorter than its diff:
```python
import jax
import jax.numpy as jnp
from jax import lax
from jax.experimental import pallas as pl
from jax.experimental.pallas import tpu as pltpu
from jax.sharding import PartitionSpec as P

D = 4096
EPSILON = 1e-05
NEGATIVE = -1e30
TOK = 128
HEAD = 128
WIDE = 256
COLS = 512
HALF = 256
NSEQ = 32
ROWS = 224
SLOTS = 256
UNITS = 352
MESH = pl.DeviceIdType.MESH
F32 = jnp.float32
BF16 = jnp.bfloat16


def dot(a, b):
    return jnp.dot(a, b, preferred_element_type=F32)


def dot_nt(a, b):
    return lax.dot_general(a, b, (((1,), (1,)), ((), ())), preferred_element_type=F32)


def iota(shape, dim):
    return lax.broadcasted_iota(jnp.int32, shape, dim)


def as_column(row):
    return jnp.transpose(jnp.broadcast_to(row, (TOK, TOK)))


def kernel(
    q_hbm, k_hbm, v_hbm, ids_ref, res_hbm, w_hbm, gain_ref, router_ref, gate_hbm, up_hbm, down_hbm,
    out_ref,
    qs, kb, vb, sb, res, w2, gu, d2, att, r1s, r1r, ss, sr, ob, rb, xb, acc, hb, r2s, r2r, yb, zb, resid,
    lsem, kv_s, kv_r, wd_s, wd_r, pair_s, pair_r, r1_s, r1_r, ss_s, ss_r, a_s, a_r, ag_s, ag_r, r2_s, r2_r, b_s, b_r,
):
    s = lax.axis_index("seq")
    e = lax.axis_index("exp")
    zh = e // 2
    c = e % 2
    other = 1 - c
    pe = zh * 2 + other
    ue = lax.rem(zh + 1, 4) * 2 + c
    de = lax.rem(zh + 3, 4) * 2 + c
    fe = lax.rem(zh + 2, 4) * 2 + c

    def far(src, dst, send, recv, to_s, to_e):
        return pltpu.make_async_remote_copy(
            src_ref=src, dst_ref=dst, send_sem=send, recv_sem=recv,
            device_id={"seq": to_s, "exp": to_e}, device_id_type=MESH,
        )

    barrier = pltpu.get_barrier_semaphore()

    @pl.loop(1, NSEQ)
    def _(i):
        pl.semaphore_signal(barrier, inc=1, device_id={"seq": lax.rem(s + i, NSEQ), "exp": e}, device_id_type=MESH)

    for i in range(1, 8):
        pl.semaphore_signal(barrier, inc=1, device_id={"seq": s, "exp": lax.rem(e + i, 8)}, device_id_type=MESH)

    loads = [
        pltpu.make_async_copy(q_hbm, qs, lsem.at[0]),
        pltpu.make_async_copy(k_hbm, kb.at[0], lsem.at[1]),
        pltpu.make_async_copy(v_hbm, vb.at[0], lsem.at[2]),
        pltpu.make_async_copy(res_hbm, res, lsem.at[3]),
    ]
    w_loads = [
        pltpu.make_async_copy(
            w_hbm.at[:, pl.ds(pl.multiple_of(z * 1024 + c * COLS, COLS), COLS)], w2.at[z, c], lsem.at[4 + z])
        for z in range(4)
    ]
    e_loads = [
        pltpu.make_async_copy(gate_hbm, gu.at[pl.ds(0, UNITS)], lsem.at[8]),
        pltpu.make_async_copy(up_hbm, gu.at[pl.ds(384, UNITS)], lsem.at[9]),
    ]
    d_loads = [
        pltpu.make_async_copy(
            down_hbm.at[:, pl.ds(pl.multiple_of(z * 1024 + c * COLS, COLS), COLS)], d2.at[z, c], lsem.at[10 + z])
        for z in range(4)
    ]
    for copy in loads + w_loads + e_loads + d_loads:
        copy.start()
    gu[UNITS:384, :] = jnp.broadcast_to(router_ref[...].astype(F32), (32, D)).astype(BF16)

    pl.semaphore_wait(barrier, NSEQ - 1 + 7)

    kv = []
    for k in range(1, 5):
        to = lax.rem(s + k, NSEQ)
        kv.append([
            far(ids_ref, sb.at[k], kv_s.at[k - 1, 0], kv_r.at[k - 1, 0], to, e),
            far(k_hbm, kb.at[k], kv_s.at[k - 1, 1], kv_r.at[k - 1, 1], to, e),
            far(v_hbm, vb.at[k], kv_s.at[k - 1, 2], kv_r.at[k - 1, 2], to, e),
        ])
    for j in range(3):
        for trio in kv:
            trio[j].start()
    wd = [
        far(w_hbm.at[:, pl.ds(pl.multiple_of(z * 1024 + other * COLS, COLS), COLS)], w2.at[z, c],
            wd_s.at[z], wd_r.at[z], s, pe)
        for z in range(4)
    ] + [
        far(down_hbm.at[:, pl.ds(pl.multiple_of(z * 1024 + other * COLS, COLS), COLS)], d2.at[z, c],
            wd_s.at[4 + z], wd_r.at[4 + z], s, pe)
        for z in range(4)
    ]
    for copy in wd:
        copy.start()

    ids = ids_ref[...].astype(F32)
    seg_row, picked_row = ids[0:1, :], ids[1:2, :]
    seg_col = as_column(seg_row)
    picked_col = as_column(picked_row)
    same = picked_col == jnp.broadcast_to(picked_row, (TOK, TOK))
    sub, lane = iota((TOK, TOK), 0), iota((TOK, TOK), 1)
    rank_row = jnp.sum(jnp.where(same & (sub < lane), 1.0, 0.0), axis=0, keepdims=True)
    rank_col = jnp.sum(jnp.where(same & (lane < sub), 1.0, 0.0), axis=1, keepdims=True)
    slot_row = picked_row * 8.0 + rank_row
    slot_col = picked_col[:, 0:1] * 8.0 + rank_col
    spread = jnp.where(iota((SLOTS, TOK), 0).astype(F32) == slot_row, 1.0, 0.0).astype(BF16)
    pick = jnp.where(iota((TOK, SLOTS), 1).astype(F32) == slot_col, 1.0, 0.0).astype(BF16)

    for copy in loads:
        copy.wait()
    scores = []
    for k in range(5):
        if k == 0:
            allowed = (seg_col == seg_row) & (lane <= sub)
        else:
            kv[k - 1][0].wait_recv()
            kv[k - 1][1].wait_recv()
            shift = jnp.where(s >= k, 0.0, 1000.0)
            allowed = seg_col == sb[k][0:1, :].astype(F32) + shift
        both = []
        for h in range(2):
            cols = slice(h * HEAD, (h + 1) * HEAD)
            raw = dot_nt(qs[:, cols], kb[k, :, cols]) * HEAD ** (-0.5)
            both.append(jnp.where(allowed, raw, NEGATIVE))
        scores.append(both)
    for k in range(1, 5):
        kv[k - 1][2].wait_recv()
    for h in range(2):
        cols = slice(h * HEAD, (h + 1) * HEAD)
        top = scores[0][h]
        for k in range(1, 5):
            top = jnp.maximum(top, scores[k][h])
        top = jnp.max(top, axis=1, keepdims=True)
        total = jnp.zeros((TOK, TOK), F32)
        numer = jnp.zeros((TOK, HEAD), F32)
        for k in range(5):
            weight = jnp.exp(scores[k][h] - top)
            total = total + weight
            numer = numer + dot(weight.astype(BF16), vb[k, :, cols])
        denom = jnp.sum(total, axis=1, keepdims=True)
        att[c, :, cols] = (numer / denom).astype(BF16)
    att_x = far(att.at[c], att.at[c], pair_s.at[0], pair_r.at[0], s, pe)
    att_x.start()
    for copy in w_loads:
        copy.wait()
    for z in range(4):
        wd[z].wait_recv()
    att_x.wait_recv()

    def reduced(part, sent, came, sends, recvs):
        def go(i, to):
            copy = far(sent.at[i], came.at[i], sends.at[i], recvs.at[i], s, to)
            copy.start()
            return copy

        value = part(lax.rem(zh + 2, 4))
        sent[0] = value[:, :HALF].astype(BF16)
        sent[3] = value[:, HALF:].astype(BF16)
        c0, c3 = go(0, ue), go(3, de)
        up_value = part(lax.rem(zh + 1, 4))
        sent[1] = up_value[:, HALF:].astype(BF16)
        c1 = go(1, ue)
        down_value = part(lax.rem(zh + 3, 4))
        sent[4] = down_value[:, :HALF].astype(BF16)
        c4 = go(4, de)
        own = part(zh)
        c0.wait_recv()
        sent[2] = (up_value[:, :HALF] + came[0].astype(F32)).astype(BF16)
        c2 = go(2, ue)
        c3.wait_recv()
        sent[5] = (down_value[:, HALF:] + came[3].astype(F32)).astype(BF16)
        c5 = go(5, de)
        for copy in (c1, c4, c2, c5):
            copy.wait_recv()
        left = own[:, :HALF] + came[2].astype(F32) + came[4].astype(F32)
        right = own[:, HALF:] + came[1].astype(F32) + came[5].astype(F32)
        return left, right, (c0, c1, c2, c3, c4, c5)

    def projected(z):
        return dot(att[0], w2[z, 0]) + dot(att[1], w2[z, 1])

    left, right, r1 = reduced(projected, r1s, r1r, r1_s, r1_r)
    left = res[:, :HALF].astype(F32) + left
    right = res[:, HALF:].astype(F32) + right
    resid[:, :HALF] = left
    resid[:, HALF:] = right

    squares = jnp.sum(left * left + right * right, axis=1, keepdims=True)
    squares = jnp.transpose(jnp.broadcast_to(squares, (TOK, TOK)))[0:8, :]
    ss[...] = squares
    sr[e] = squares
    ss_x = []
    for i in range(1, 8):
        copy = far(ss, sr.at[e], ss_s.at[i - 1], ss_r.at[0], s, lax.rem(e + i, 8))
        copy.start()
        ss_x.append(copy)
    pltpu.make_async_copy(sr.at[pl.ds(0, 7)], sr.at[pl.ds(0, 7)], ss_r.at[0]).wait()
    sum_row = jnp.sum(sr[...], axis=0)[0:1, :]
    scale = as_column(lax.rsqrt(sum_row / D + EPSILON))[:, 0:1]
    normed = (resid[...] * scale * gain_ref[...]).astype(BF16)

    ob[...] = dot(spread, normed).reshape(NSEQ, 8, COLS).astype(BF16)
    rb[s] = ob[s]

    @pl.loop(1, NSEQ)
    def _(i):
        to = lax.rem(s + i, NSEQ)
        far(ob.at[to], rb.at[s], a_s.at[0], a_r.at[0], to, e).start()

    pltpu.make_async_copy(ob.at[pl.ds(0, NSEQ - 1)], rb.at[pl.ds(0, NSEQ - 1)], a_r.at[0]).wait()
    row, col = iota((ROWS, SLOTS), 0), iota((ROWS, SLOTS), 1)
    tight = jnp.where((row == (col >> 3) * 7 + (col & 7)) & ((col & 7) < 7), 1.0, 0.0).astype(BF16)
    row, col = iota((SLOTS, ROWS), 0), iota((SLOTS, ROWS), 1)
    loose = jnp.where((col == (row >> 3) * 7 + (row & 7)) & ((row & 7) < 7), 1.0, 0.0).astype(BF16)
    xb[e] = dot(tight, rb[...].astype(F32).reshape(SLOTS, COLS).astype(BF16)).astype(BF16)

    first, second = pl.ds(0, ROWS // 2), pl.ds(ROWS // 2, ROWS // 2)

    def pass_on(i, src_e, rows, to):
        return far(xb.at[src_e, rows], xb.at[src_e, rows], ag_s.at[i], ag_r.at[i], s, to)

    def share(i, src_e):
        return far(xb.at[src_e], xb.at[src_e], ag_s.at[i], ag_r.at[i], s, pe)

    g0, g2 = pass_on(0, e, first, ue), pass_on(2, e, second, de)
    g1, g3 = pass_on(1, e, second, ue), pass_on(3, e, first, de)
    g4, g5 = pass_on(4, de, first, ue), pass_on(5, ue, second, de)
    g6, g7, g8, g9 = share(6, e), share(7, de), share(8, ue), share(9, fe)
    for copy in (g0, g2, g6, g1, g3):
        copy.start()

    def absorb(src_e):
        return dot_nt(xb[src_e], gu[:, pl.ds(pl.multiple_of(src_e * COLS, COLS), COLS)])

    def flip(src_e):
        return src_e + 1 - 2 * c

    for copy in e_loads:
        copy.wait()
    acc[...] = absorb(e)
    g6.wait_recv()
    acc[...] += absorb(pe)
    g0.wait_recv()
    g4.start()
    g2.wait_recv()
    g5.start()
    g1.wait_recv()
    g7.start()
    g3.wait_recv()
    g8.start()
    acc[...] += absorb(de)
    acc[...] += absorb(ue)
    g7.wait_recv()
    acc[...] += absorb(flip(de))
    g8.wait_recv()
    acc[...] += absorb(flip(ue))
    g4.wait_recv()
    g5.wait_recv()
    g9.start()
    acc[...] += absorb(fe)
    g9.wait_recv()
    acc[...] += absorb(flip(fe))

    gate_sum = acc[:, 0:UNITS]
    up_sum = acc[:, 384:384 + UNITS]
    logit = acc[:, UNITS:UNITS + 1]
    hidden = gate_sum / (1.0 + jnp.exp(-gate_sum)) * up_sum * (1.0 / (1.0 + jnp.exp(-logit)))
    hb[c] = hidden.astype(BF16)
    hid_x = far(hb.at[c], hb.at[c], pair_s.at[1], pair_r.at[1], s, pe)
    hid_x.start()
    for copy in d_loads:
        copy.wait()
    for z in range(4, 8):
        wd[z].wait_recv()
    hid_x.wait_recv()

    def expert_out(z):
        return dot(hb[0], d2[z, 0]) + dot(hb[1], d2[z, 1])

    left, right, r2 = reduced(expert_out, r2s, r2r, r2_s, r2_r)
    yb[:, :, :HALF] = dot(loose, left.astype(BF16)).reshape(NSEQ, 8, HALF).astype(BF16)
    yb[:, :, HALF:] = dot(loose, right.astype(BF16)).reshape(NSEQ, 8, HALF).astype(BF16)
    zb[s] = yb[s]

    @pl.loop(1, NSEQ)
    def _(i):
        to = lax.rem(s + i, NSEQ)
        far(yb.at[to], zb.at[s], b_s.at[0], b_r.at[0], to, e).start()

    pltpu.make_async_copy(yb.at[pl.ds(0, NSEQ - 1)], zb.at[pl.ds(0, NSEQ - 1)], b_r.at[0]).wait()
    routed = dot(pick, zb[...].astype(F32).reshape(SLOTS, COLS).astype(BF16))
    out_ref[...] = (resid[...] + routed).astype(BF16)

    for trio in kv:
        for copy in trio:
            copy.wait_send()
    for copy in wd + [att_x, hid_x, *r1, *r2, *ss_x, g0, g1, g2, g3, g4, g5, g6, g7, g8, g9]:
        copy.wait_send()
    for buf, sem in ((ob, a_s), (yb, b_s)):
        pltpu.make_async_copy(buf.at[pl.ds(0, NSEQ - 1)], buf.at[pl.ds(0, NSEQ - 1)], sem.at[0]).wait()


def local(
    query_input, key_input, value_input, segment_ids, residual_in, out_weight, norm_gain, router,
    modality, expert_in, gate_weight, up_weight, down_weight,
):
    ids = jnp.concatenate([
        segment_ids[None], (modality * 16 + expert_in)[None], jnp.zeros((6, TOK), jnp.int32)
    ])
    anywhere = pl.BlockSpec(memory_space=pl.ANY)
    vmem = pl.BlockSpec(memory_space=pltpu.VMEM)
    V = pltpu.VMEM
    dma = pltpu.SemaphoreType.DMA
    return pl.pallas_call(
        kernel,
        out_shape=jax.ShapeDtypeStruct((TOK, COLS), BF16),
        in_specs=[anywhere, anywhere, anywhere, vmem, anywhere, anywhere, vmem, vmem, anywhere, anywhere, anywhere],
        out_specs=vmem,
        scratch_shapes=[
            V((TOK, WIDE), BF16),
            V((5, TOK, WIDE), BF16),
            V((5, TOK, WIDE), BF16),
            V((5, 8, TOK), jnp.int32),
            V((TOK, COLS), BF16),
            V((4, 2, WIDE, COLS), BF16),
            V((736, D), BF16),
            V((4, 2, UNITS, COLS), BF16),
            V((2, TOK, WIDE), BF16),
            V((6, TOK, HALF), BF16),
            V((6, TOK, HALF), BF16),
            V((8, TOK), F32),
            V((8, 8, TOK), F32),
            V((NSEQ, 8, COLS), BF16),
            V((NSEQ, 8, COLS), BF16),
            V((8, ROWS, COLS), BF16),
            V((ROWS, 736), F32),
            V((2, ROWS, UNITS), BF16),
            V((6, ROWS, HALF), BF16),
            V((6, ROWS, HALF), BF16),
            V((NSEQ, 8, COLS), BF16),
            V((NSEQ, 8, COLS), BF16),
            V((TOK, COLS), F32),
            dma((14,)),
            dma((4, 3)), dma((4, 3)),
            dma((8,)), dma((8,)),
            dma((2,)), dma((2,)),
            dma((6,)), dma((6,)),
            dma((7,)), dma((1,)),
            dma((1,)), dma((1,)),
            dma((10,)), dma((10,)),
            dma((6,)), dma((6,)),
            dma((1,)), dma((1,)),
        ],
        compiler_params=pltpu.CompilerParams(
            collective_id=0, has_side_effects=True, vmem_limit_bytes=60 * 1024 * 1024),
    )(
        query_input, key_input, value_input, ids, residual_in, out_weight, norm_gain.reshape(1, COLS),
        router.T, gate_weight[0].T, up_weight[0].T, down_weight[0],
    )


def solution(mesh):
    placed = (
        P("seq", "exp"), P("seq", "exp"), P("seq", "exp"), P("seq"), P("seq", "exp"), P("exp", None), P("exp"),
        P(None, "seq"), P("seq"), P("seq"), P("seq", None, "exp"), P("seq", None, "exp"), P("seq", "exp", None),
    )
    return jax.shard_map(local, mesh=mesh, in_specs=placed, out_specs=P("seq", "exp"), check_vma=False)
```

time: 267 us -> 96.6 us (0.36)
  waiting for transfers between devices: 95.8 us -> 0 us
  Pallas kernels: 0 us -> 92.7 us
  starting transfers between devices: 75.3 us -> 0 us
  blocking collectives: 36 us -> 0 us
  local copies, waits for them, and re-layouts: 18 us -> 1.65 us
  between operations: 13.6 us -> 0.01 us
  matrix products: 12.9 us -> 0 us
  other arithmetic: 12.6 us -> 1.99 us
    pallas_call x0 -> x1, Pallas kernels: none -> 92.7 us  [local(): pl.pallas_call(kernel, out_shape=jax.ShapeDtypeStruct((TOK, COLS), BF16),...]
    reduce_scatter x1 -> x0, waiting for transfers between devices: 41.8 us -> none  [local(): lax.psum_scatter(partial_value.astype(jnp.bfloat16), EXP, scatter_dimensi...]
    ppermute x12 -> x0, starting transfers between devices: 41.1 us -> none  [passed_along(): lax.ppermute(value, axis, [(source, source + steps) for source in range(l...]
    all_to_all x3 -> x0, waiting for transfers between devices: 35.9 us -> none  [the longest x1 21.1 us: sent_and_summed(): tiles = lax.all_to_all(split_up(array, dim, length), axis, 0, 0, tiled=True)]
    all_to_all x3 -> x0, starting transfers between devices: 34.1 us -> none  [the longest x1 15.5 us: sent_and_summed(): tiles = lax.all_to_all(split_up(array, dim, length), axis, 0, 0, tiled=True)]
    all_to_all x1 -> x0, blocking collectives: 18.8 us -> none  [local(): lax.all_to_all(outgoing.reshape(EXPERTS, CAPACITY, normed.shape[1]), 'seq...]
    all_gather x1 -> x0, blocking collectives: 17.2 us -> none  [stacked_from(): tiles = lax.all_gather(tiles, axes[k])]
    all_gather x1 -> x0, waiting for transfers between devices: 16.6 us -> none  [stacked_from(): tiles = lax.all_gather(tiles, axes[k])]
  transfers between devices with their start and end apart: 17 -> 0, of which waited for: 9 -> 0; matrix products, arithmetic and copies ran while one was open for 2% -> 0% of each run, Pallas kernels for 0% -> 0%
where the time goes in v1:
time: 96.6 us; the launch traced here: 96.4 us
  Pallas kernels  92.7 us (96%)
  other arithmetic  1.99 us (2%)
  local copies, waits for them, and re-layouts  1.65 us (2%)
    pallas_call x1, Pallas kernels, local(): pl.pallas_call(kernel, out_shape=jax.ShapeDtypeStruct((TOK, COLS), BF16),...  92.7 us

profile of v1, /device:TPU:1, one launch (start us, length us, event | category | flops | bytes accessed | tf_op | source)
XLA Modules:
  0.0 96.4 jit_solution(11703793451419872150)
XLA Ops:
  0.0 0.7 add_bitcast_fusion
  0.7 0.1 pad.2.clone
  0.8 1.3 %add_add_fusion.ids_ref = s32[8,128]{1,0:T(8,128)} fusion(s32[1,128]{1,0:T(1,128)S(1)} %add_bitcast_fusion, s32[1,128]{1,0:T(1,128)} %bitcast.17, s32[8]{0:T(128)S(1)} %pad.2.clone), kind=kLoop, calls=%fused_computation | loop fusion | flops 2048 | bytes 5152 | tf_op jit(solution)/shard_map/concatenate | solution.py:332
  2.1 92.7 %shard_map.127 = bf16[128,512]{1,0:T(8,128)(2,1)} custom-call(bf16[128,256]{1,0:T(8,128)(2,1)} %q_hbm.1, bf16[128,256]{1,0:T(8,128)(2,1)} %k_hbm.1, bf16[128,256]{1,0:T(8,128)(2,1)} %v_hbm.1, s32[8,128]{1,0:T(8,128)} %add_add_fusion.ids_ref, bf16[128,512]{1,0:T(8,128)(2,1)} %res_hbm.1, bf16[256,4096]{1,0:T(8,128)(2,1)} %w_hbm.1, f32[1,512]{1,0:T(1,128)} %bitcast.16, ...), custom_call_target="tpu_custom_call" | custom-call | tf_op jit(solution)/shard_map/pallas_call | solution.py:339
  94.8 1.6 %copy.15 = bf16[128,512]{1,0:T(8,128)(2,1)} copy(bf16[128,512]{1,0:T(8,128)(2,1)} %shard_map.127) | data formatting | bytes 262144
  (1 shorter events, 0.0 us)

commit v2 on v1

--- a/solution.py
+++ b/solution.py
@@ -39,10 +39,10 @@
 
 
 def kernel(
-    q_hbm, k_hbm, v_hbm, ids_ref, res_hbm, w_hbm, gain_ref, router_ref, gate_hbm, up_hbm, down_hbm,
+    q_hbm, k_hbm, v_hbm, seg_hbm, mod_hbm, pick_hbm, res_hbm, w_hbm, gain_hbm, router_hbm, gate_hbm, up_hbm, down_hbm,
     out_ref,
-    qs, kb, vb, sb, res, w2, gu, d2, att, r1s, r1r, ss, sr, ob, rb, xb, acc, hb, r2s, r2r, yb, zb, resid,
-    lsem, kv_s, kv_r, wd_s, wd_r, pair_s, pair_r, r1_s, r1_r, ss_s, ss_r, a_s, a_r, ag_s, ag_r, r2_s, r2_r, b_s, b_r,
+    qs, kb, vb, sb, mods, picks, gains, rout, res, w2, gu, d2, att, r1s, r1r, ss, sr, ob, rb, osc, rsc, xb, acc, hb,
+    r2s, r2r, yb, zb, resid, known, lsem, kv_s, kv_r, wd_s, wd_r, pair_s, pair_r, r1_s, r1_r, ss_s, ss_r, a_s, a_r, c_s, c_r, ag_s, ag_r, r2_s, r2_r, b_s, b_r,
 ):
     s = lax.axis_index("seq")
     e = lax.axis_index("exp")
@@ -60,19 +60,29 @@
             device_id={"seq": to_s, "exp": to_e}, device_id_type=MESH,
         )
 
+    def ring(i):
+        return lax.rem(s + i + NSEQ, NSEQ)
+
+    def tell(sem, to_s, to_e):
+        pl.semaphore_signal(sem, inc=1, device_id={"seq": to_s, "exp": to_e}, device_id_type=MESH)
+
     barrier = pltpu.get_barrier_semaphore()
-
-    @pl.loop(1, NSEQ)
-    def _(i):
-        pl.semaphore_signal(barrier, inc=1, device_id={"seq": lax.rem(s + i, NSEQ), "exp": e}, device_id_type=MESH)
-
-    for i in range(1, 8):
-        pl.semaphore_signal(barrier, inc=1, device_id={"seq": s, "exp": lax.rem(e + i, 8)}, device_id_type=MESH)
+    for i in (1, 2, 3, 4, -1, -2, -3, -4):
+        tell(barrier, ring(i), e)
+    for to in (pe, ue, de):
+        tell(barrier, s, to)
 
     loads = [
         pltpu.make_async_copy(q_hbm, qs, lsem.at[0]),
         pltpu.make_async_copy(k_hbm, kb.at[0], lsem.at[1]),
         pltpu.make_async_copy(v_hbm, vb.at[0], lsem.at[2]),
+        pltpu.make_async_copy(seg_hbm, sb.at[0], lsem.at[14]),
+    ]
+    later = [
+        pltpu.make_async_copy(mod_hbm, mods, lsem.at[15]),
+        pltpu.make_async_copy(pick_hbm, picks, lsem.at[16]),
+        pltpu.make_async_copy(gain_hbm, gains, lsem.at[17]),
+        pltpu.make_async_copy(router_hbm, rout, lsem.at[18]),
         pltpu.make_async_copy(res_hbm, res, lsem.at[3]),
     ]
     w_loads = [
@@ -89,19 +99,19 @@
             down_hbm.at[:, pl.ds(pl.multiple_of(z * 1024 + c * COLS, COLS), COLS)], d2.at[z, c], lsem.at[10 + z])
         for z in range(4)
     ]
-    for copy in loads + w_loads + e_loads + d_loads:
+    for copy in loads + later + w_loads + e_loads + d_loads:
         copy.start()
-    gu[UNITS:384, :] = jnp.broadcast_to(router_ref[...].astype(F32), (32, D)).astype(BF16)
-
-    pl.semaphore_wait(barrier, NSEQ - 1 + 7)
+    for copy in loads:
+        copy.wait()
+    pl.semaphore_wait(barrier, 11)
 
     kv = []
     for k in range(1, 5):
-        to = lax.rem(s + k, NSEQ)
+        to = ring(k)
         kv.append([
-            far(ids_ref, sb.at[k], kv_s.at[k - 1, 0], kv_r.at[k - 1, 0], to, e),
-            far(k_hbm, kb.at[k], kv_s.at[k - 1, 1], kv_r.at[k - 1, 1], to, e),
-            far(v_hbm, vb.at[k], kv_s.at[k - 1, 2], kv_r.at[k - 1, 2], to, e),
+            far(sb.at[0], sb.at[k], kv_s.at[k - 1, 0], kv_r.at[k - 1, 0], to, e),
+            far(kb.at[0], kb.at[k], kv_s.at[k - 1, 1], kv_r.at[k - 1, 1], to, e),
+            far(vb.at[0], vb.at[k], kv_s.at[k - 1, 2], kv_r.at[k - 1, 2], to, e),
         ])
     for j in range(3):
         for trio in kv:
@@ -115,11 +125,15 @@
             wd_s.at[4 + z], wd_r.at[4 + z], s, pe)
         for z in range(4)
     ]
+    tell(known.at[0], ring(4), e)
+    tell(known.at[0], ring(-4), e)
     for copy in wd:
         copy.start()
 
-    ids = ids_ref[...].astype(F32)
-    seg_row, picked_row = ids[0:1, :], ids[1:2, :]
+    for copy in later:
+        copy.wait()
+    gu[UNITS:384, :] = jnp.broadcast_to(rout[...].astype(F32), (32, D)).astype(BF16)
+    seg_row, picked_row = sb[0].astype(F32), (mods[...] * 16 + picks[...]).astype(F32)
     seg_col = as_column(seg_row)
     picked_col = as_column(picked_row)
     same = picked_col == jnp.broadcast_to(picked_row, (TOK, TOK))
@@ -131,8 +145,10 @@
     spread = jnp.where(iota((SLOTS, TOK), 0).astype(F32) == slot_row, 1.0, 0.0).astype(BF16)
     pick = jnp.where(iota((TOK, SLOTS), 1).astype(F32) == slot_col, 1.0, 0.0).astype(BF16)
 
-    for copy in loads:
-        copy.wait()
+    pl.semaphore_wait(known.at[0], 2)
+    tell(known.at[1], ring(8), e)
+    tell(known.at[1], ring(-8), e)
+
     scores = []
     for k in range(5):
         if k == 0:
@@ -141,7 +157,7 @@
             kv[k - 1][0].wait_recv()
             kv[k - 1][1].wait_recv()
             shift = jnp.where(s >= k, 0.0, 1000.0)
-            allowed = seg_col == sb[k][0:1, :].astype(F32) + shift
+            allowed = seg_col == sb[k].astype(F32) + shift
         both = []
         for h in range(2):
             cols = slice(h * HEAD, (h + 1) * HEAD)
@@ -210,27 +226,29 @@
     resid[:, :HALF] = left
     resid[:, HALF:] = right
 
-    squares = jnp.sum(left * left + right * right, axis=1, keepdims=True)
-    squares = jnp.transpose(jnp.broadcast_to(squares, (TOK, TOK)))[0:8, :]
-    ss[...] = squares
-    sr[e] = squares
-    ss_x = []
-    for i in range(1, 8):
-        copy = far(ss, sr.at[e], ss_s.at[i - 1], ss_r.at[0], s, lax.rem(e + i, 8))
-        copy.start()
-        ss_x.append(copy)
-    pltpu.make_async_copy(sr.at[pl.ds(0, 7)], sr.at[pl.ds(0, 7)], ss_r.at[0]).wait()
-    sum_row = jnp.sum(sr[...], axis=0)[0:1, :]
-    scale = as_column(lax.rsqrt(sum_row / D + EPSILON))[:, 0:1]
-    normed = (resid[...] * scale * gain_ref[...]).astype(BF16)
-
-    ob[...] = dot(spread, normed).reshape(NSEQ, 8, COLS).astype(BF16)
-    rb[s] = ob[s]
+    pl.semaphore_wait(known.at[1], 2)
+
+    gained = (resid[...] * gains[...]).astype(BF16)
+    ob[...] = dot(spread, gained).reshape(NSEQ, 8, COLS).astype(BF16)
 
     @pl.loop(1, NSEQ)
     def _(i):
         to = lax.rem(s + i, NSEQ)
         far(ob.at[to], rb.at[s], a_s.at[0], a_r.at[0], to, e).start()
+
+    rb[s] = ob[s]
+
+    squares = jnp.sum(left * left + right * right, axis=1, keepdims=True)
+    squares = jnp.transpose(jnp.broadcast_to(squares, (TOK, TOK)))[0:8, :]
+    ss[0] = squares
+    ss_p = far(ss.at[0], sr.at[0], ss_s.at[0], ss_r.at[0], s, pe)
+    ss_p.start()
+    ss_p.wait_recv()
+    squares = squares + sr[0]
+    ss[1] = squares
+    ss_z = [far(ss.at[1], sr.at[i], ss_s.at[i], ss_r.at[i], s, to) for i, to in ((1, ue), (2, de), (3, fe))]
+    for copy in ss_z:
+        copy.start()
 
     pltpu.make_async_copy(ob.at[pl.ds(0, NSEQ - 1)], rb.at[pl.ds(0, NSEQ - 1)], a_r.at[0]).wait()
     row, col = iota((ROWS, SLOTS), 0), iota((ROWS, SLOTS), 1)
@@ -253,6 +271,19 @@
     g6, g7, g8, g9 = share(6, e), share(7, de), share(8, ue), share(9, fe)
     for copy in (g0, g2, g6, g1, g3):
         copy.start()
+
+    for copy in ss_z:
+        copy.wait_recv()
+    scale_row = lax.rsqrt((squares + sr[1] + sr[2] + sr[3])[0:1, :] / D + EPSILON)
+    slot_scale = jnp.sum(spread.astype(F32) * scale_row, axis=1, keepdims=True)
+    osc[...] = jnp.broadcast_to(slot_scale, (SLOTS, TOK)).reshape(NSEQ, 8, TOK)
+
+    @pl.loop(1, NSEQ)
+    def _(i):
+        to = lax.rem(s + i, NSEQ)
+        far(osc.at[to], rsc.at[s], c_s.at[0], c_r.at[0], to, e).start()
+
+    rsc[s] = osc[s]
 
     def absorb(src_e):
         return dot_nt(xb[src_e], gu[:, pl.ds(pl.multiple_of(src_e * COLS, COLS), COLS)])
@@ -286,9 +317,13 @@
     g9.wait_recv()
     acc[...] += absorb(flip(fe))
 
-    gate_sum = acc[:, 0:UNITS]
-    up_sum = acc[:, 384:384 + UNITS]
-    logit = acc[:, UNITS:UNITS + 1]
+    pltpu.make_async_copy(osc.at[pl.ds(0, NSEQ - 1)], rsc.at[pl.ds(0, NSEQ - 1)], c_r.at[0]).wait()
+    scale = lax.dot_general(
+        tight.astype(F32), rsc[...].reshape(SLOTS, TOK), (((1,), (0,)), ((), ())),
+        precision=lax.Precision.HIGHEST, preferred_element_type=F32)[:, 0:1]
+    gate_sum = acc[:, 0:UNITS] * scale
+    up_sum = acc[:, 384:384 + UNITS] * scale
+    logit = acc[:, UNITS:UNITS + 1] * scale
     hidden = gate_sum / (1.0 + jnp.exp(-gate_sum)) * up_sum * (1.0 / (1.0 + jnp.exp(-logit)))
     hb[c] = hidden.astype(BF16)
     hid_x = far(hb.at[c], hb.at[c], pair_s.at[1], pair_r.at[1], s, pe)
@@ -314,14 +349,14 @@
 
     pltpu.make_async_copy(yb.at[pl.ds(0, NSEQ - 1)], zb.at[pl.ds(0, NSEQ - 1)], b_r.at[0]).wait()
     routed = dot(pick, zb[...].astype(F32).reshape(SLOTS, COLS).astype(BF16))
-    out_ref[...] = (resid[...] + routed).astype(BF16)
+    out_ref[...] = resid[...] + routed
 
     for trio in kv:
         for copy in trio:
             copy.wait_send()
-    for copy in wd + [att_x, hid_x, *r1, *r2, *ss_x, g0, g1, g2, g3, g4, g5, g6, g7, g8, g9]:
+    for copy in wd + [att_x, hid_x, *r1, *r2, ss_p, *ss_z, g0, g1, g2, g3, g4, g5, g6, g7, g8, g9]:
         copy.wait_send()
-    for buf, sem in ((ob, a_s), (yb, b_s)):
+    for buf, sem in ((ob, a_s), (osc, c_s), (yb, b_s)):
         pltpu.make_async_copy(buf.at[pl.ds(0, NSEQ - 1)], buf.at[pl.ds(0, NSEQ - 1)], sem.at[0]).wait()
 
 
@@ -329,23 +364,24 @@
     query_input, key_input, value_input, segment_ids, residual_in, out_weight, norm_gain, router,
     modality, expert_in, gate_weight, up_weight, down_weight,
 ):
-    ids = jnp.concatenate([
-        segment_ids[None], (modality * 16 + expert_in)[None], jnp.zeros((6, TOK), jnp.int32)
-    ])
-    anywhere = pl.BlockSpec(memory_space=pl.ANY)
+    anywhere = pl.BlockSpec(memory_space=pltpu.HBM)
     vmem = pl.BlockSpec(memory_space=pltpu.VMEM)
     V = pltpu.VMEM
     dma = pltpu.SemaphoreType.DMA
-    return pl.pallas_call(
+    total = pl.pallas_call(
         kernel,
-        out_shape=jax.ShapeDtypeStruct((TOK, COLS), BF16),
-        in_specs=[anywhere, anywhere, anywhere, vmem, anywhere, anywhere, vmem, vmem, anywhere, anywhere, anywhere],
+        out_shape=pltpu.VMEM((TOK, COLS), F32),
+        in_specs=[anywhere] * 13,
         out_specs=vmem,
         scratch_shapes=[
             V((TOK, WIDE), BF16),
             V((5, TOK, WIDE), BF16),
             V((5, TOK, WIDE), BF16),
-            V((5, 8, TOK), jnp.int32),
+            V((5, 1, TOK), jnp.int32),
+            V((1, TOK), jnp.int32),
+            V((1, TOK), jnp.int32),
+            V((1, COLS), F32),
+            V((1, D), BF16),
             V((TOK, COLS), BF16),
             V((4, 2, WIDE, COLS), BF16),
             V((736, D), BF16),
@@ -353,10 +389,12 @@
             V((2, TOK, WIDE), BF16),
             V((6, TOK, HALF), BF16),
             V((6, TOK, HALF), BF16),
-            V((8, TOK), F32),
-            V((8, 8, TOK), F32),
+            V((2, 8, TOK), F32),
+            V((4, 8, TOK), F32),
             V((NSEQ, 8, COLS), BF16),
             V((NSEQ, 8, COLS), BF16),
+            V((NSEQ, 8, TOK), F32),
+            V((NSEQ, 8, TOK), F32),
             V((8, ROWS, COLS), BF16),
             V((ROWS, 736), F32),
             V((2, ROWS, UNITS), BF16),
@@ -365,23 +403,27 @@
             V((NSEQ, 8, COLS), BF16),
             V((NSEQ, 8, COLS), BF16),
             V((TOK, COLS), F32),
-            dma((14,)),
+            pltpu.SemaphoreType.REGULAR((2,)),
+            dma((19,)),
             dma((4, 3)), dma((4, 3)),
             dma((8,)), dma((8,)),
             dma((2,)), dma((2,)),
             dma((6,)), dma((6,)),
-            dma((7,)), dma((1,)),
+            dma((4,)), dma((4,)),
+            dma((1,)), dma((1,)),
             dma((1,)), dma((1,)),
             dma((10,)), dma((10,)),
             dma((6,)), dma((6,)),
             dma((1,)), dma((1,)),
         ],
         compiler_params=pltpu.CompilerParams(
-            collective_id=0, has_side_effects=True, vmem_limit_bytes=60 * 1024 * 1024),
+            collective_id=0, has_side_effects=True, vmem_limit_bytes=67043328 - 278528),
     )(
-        query_input, key_input, value_input, ids, residual_in, out_weight, norm_gain.reshape(1, COLS),
+        query_input, key_input, value_input, segment_ids.reshape(1, TOK), modality.reshape(1, TOK),
+        expert_in.reshape(1, TOK), residual_in, out_weight, norm_gain.reshape(1, COLS),
         router.T, gate_weight[0].T, up_weight[0].T, down_weight[0],
     )
+    return total.astype(BF16)
 
 
 def solution(mesh):

time: 96.6 us -> 89 us (0.921)
  Pallas kernels: 92.7 us -> 88.3 us
  local copies, waits for them, and re-layouts: 1.65 us -> 0 us
  other arithmetic: 1.99 us -> 0.67 us
    pallas_call x1, Pallas kernels: 92.7 us -> 88.3 us  [local(): pl.pallas_call(kernel, out_shape=pltpu.VMEM((TOK, COLS), F32), in_specs=[...]
    unnamed x1 -> x0, local copies, waits for them, and re-layouts: 1.57 us -> none
    concatenate x1 -> x0, other arithmetic: 1.32 us -> none  [local(): jnp.concatenate([segment_ids[None], (modality * 16 + expert_in)[None], jn...]
where the time goes in v2:
time: 89 us; the launch traced here: 88.9 us
  Pallas kernels  88.3 us (99%)
    pallas_call x1, Pallas kernels, local(): pl.pallas_call(kernel, out_shape=pltpu.VMEM((TOK, COLS), F32), in_specs=[...  88.3 us

profile of v2, /device:TPU:1, one launch (start us, length us, event | category | flops | bytes accessed | tf_op | source)
XLA Modules:
  0.0 88.9 jit_solution(2489218008363733034)
XLA Ops:
  0.0 88.3 %shard_map.127 = f32[128,512]{1,0:T(8,128)S(1)} custom-call(bf16[128,256]{1,0:T(8,128)(2,1)} %q_hbm.1, bf16[128,256]{1,0:T(8,128)(2,1)} %k_hbm.1, bf16[128,256]{1,0:T(8,128)(2,1)} %v_hbm.1, s32[1,128]{1,0:T(1,128)} %bitcast.17, s32[1,128]{1,0:T(1,128)} %bitcast.18, s32[1,128]{1,0:T(1,128)} %bitcast.19, bf16[128,512]{1,0:T(8,128)(2,1)} %res_hbm.1, ...), custom_call_target="tpu_custom_call" | custom-call | tf_op jit(solution)/shard_map/pallas_call | solution.py:371
  88.3 0.7 convert_element_type.3

commit v3 on v2

v3 whole, which is shorter than its diff:
```python
import jax
import jax.numpy as jnp
from jax import lax
from jax.experimental import pallas as pl
from jax.experimental.pallas import tpu as pltpu
from jax.sharding import PartitionSpec as P

D = 4096
EPSILON = 1e-05
NEGATIVE = -1e30
TOK = 128
HEAD = 128
WIDE = 256
COLS = 512
HALF = 256
QUART = 128
NSEQ = 32
ROWS = 224
SLOTS = 256
UNITS = 352
MESH = pl.DeviceIdType.MESH
F32 = jnp.float32
BF16 = jnp.bfloat16


def dot(a, b):
    return jnp.dot(a, b, preferred_element_type=F32)


def dot_nt(a, b):
    return lax.dot_general(a, b, (((1,), (1,)), ((), ())), preferred_element_type=F32)


def exact_dot(a, b):
    return jnp.dot(a, b, precision=lax.Precision.HIGHEST, preferred_element_type=F32)


def iota(shape, dim):
    return lax.broadcasted_iota(jnp.int32, shape, dim)


def as_column(row):
    return jnp.transpose(jnp.broadcast_to(row, (TOK, TOK)))


def kernel(
    q_hbm, k_hbm, v_hbm, seg_hbm, mod_hbm, pick_hbm, res_hbm, w_hbm, gain_hbm, router_hbm, gate_hbm, up_hbm, down_hbm,
    out_ref,
    qs, kb, vb, sb, mods, picks, gains, rout, res, w2, gu, d2, att, r1s, r1r, ss, sr, ob, rb, osc, rsc, xb, acc, hb,
    r2s, r2r, yb, zb, resid, known, lsem, kv_s, kv_r, wd_s, wd_r, pair_s, pair_r, r1_s, r1_r, ss_s, ss_r, a_s, a_r, c_s, c_r, ag_s, ag_r, r2_s, r2_r, b_s, b_r,
):
    s = lax.axis_index("seq")
    e = lax.axis_index("exp")
    zh = e // 2
    c = e % 2
    other = 1 - c
    pe = zh * 2 + other
    ue = lax.rem(zh + 1, 4) * 2 + c
    de = lax.rem(zh + 3, 4) * 2 + c
    fe = lax.rem(zh + 2, 4) * 2 + c
    pfe = lax.rem(zh + 2, 4) * 2 + other

    def far(src, dst, send, recv, to_s, to_e):
        return pltpu.make_async_remote_copy(
            src_ref=src, dst_ref=dst, send_sem=send, recv_sem=recv,
            device_id={"seq": to_s, "exp": to_e}, device_id_type=MESH,
        )

    def ring(i):
        return lax.rem(s + i + NSEQ, NSEQ)

    def tell(sem, to_s, to_e):
        pl.semaphore_signal(sem, inc=1, device_id={"seq": to_s, "exp": to_e}, device_id_type=MESH)

    barrier = pltpu.get_barrier_semaphore()
    for i in (1, 2, 3, 4, -1, -2, -3, -4):
        tell(barrier, ring(i), e)
    for to in (pe, ue, de):
        tell(barrier, s, to)

    loads = [
        pltpu.make_async_copy(q_hbm, qs, lsem.at[0]),
        pltpu.make_async_copy(k_hbm, kb.at[0], lsem.at[1]),
        pltpu.make_async_copy(v_hbm, vb.at[0], lsem.at[2]),
        pltpu.make_async_copy(seg_hbm, sb.at[0], lsem.at[14]),
    ]
    later = [
        pltpu.make_async_copy(mod_hbm, mods, lsem.at[15]),
        pltpu.make_async_copy(pick_hbm, picks, lsem.at[16]),
        pltpu.make_async_copy(gain_hbm, gains, lsem.at[17]),
        pltpu.make_async_copy(router_hbm, rout, lsem.at[18]),
        pltpu.make_async_copy(res_hbm, res, lsem.at[3]),
    ]
    w_loads = [
        pltpu.make_async_copy(
            w_hbm.at[:, pl.ds(pl.multiple_of(z * 1024 + c * COLS, COLS), COLS)], w2.at[z, c], lsem.at[4 + z])
        for z in range(4)
    ]
    e_loads = [
        pltpu.make_async_copy(gate_hbm, gu.at[pl.ds(0, UNITS)], lsem.at[8]),
        pltpu.make_async_copy(up_hbm, gu.at[pl.ds(384, UNITS)], lsem.at[9]),
    ]
    d_loads = [
        pltpu.make_async_copy(
            down_hbm.at[:, pl.ds(pl.multiple_of(z * 1024 + c * COLS, COLS), COLS)], d2.at[z, c], lsem.at[10 + z])
        for z in range(4)
    ]
    for copy in loads + later + w_loads + e_loads + d_loads:
        copy.start()
    for copy in loads:
        copy.wait()
    pl.semaphore_wait(barrier, 11)

    last = lax.rem(s, 4) == 3

    def trio_of(k, src, to):
        return [
            far(buf.at[src], buf.at[k], kv_s.at[k - 1, j], kv_r.at[k - 1, j], to, e)
            for j, buf in enumerate((sb, kb, vb))
        ]

    kv = [trio_of(k, 0, ring(k)) for k in range(1, 5)]
    relay = trio_of(1, 4, ring(-3))
    for k in (4, 3, 2):
        kv[k - 1][0].start()
    for k in (4, 3, 2):
        kv[k - 1][1].start()
        kv[k - 1][2].start()

    @pl.when(jnp.logical_not(last))
    def _():
        for copy in kv[0]:
            copy.start()

    wd = [
        far(w_hbm.at[:, pl.ds(pl.multiple_of(z * 1024 + other * COLS, COLS), COLS)], w2.at[z, c],
            wd_s.at[z], wd_r.at[z], s, pe)
        for z in range(4)
    ] + [
        far(down_hbm.at[:, pl.ds(pl.multiple_of(z * 1024 + other * COLS, COLS), COLS)], d2.at[z, c],
            wd_s.at[4 + z], wd_r.at[4 + z], s, pe)
        for z in range(4)
    ]
    tell(known.at[0], ring(4), e)
    tell(known.at[0], ring(-4), e)
    for copy in wd:
        copy.start()

    for copy in later:
        copy.wait()
    gu[UNITS:384, :] = jnp.broadcast_to(rout[...].astype(F32), (32, D)).astype(BF16)
    seg_row, picked_row = sb[0].astype(F32), (mods[...] * 16 + picks[...]).astype(F32)
    seg_col = as_column(seg_row)
    picked_col = as_column(picked_row)
    same = picked_col == jnp.broadcast_to(picked_row, (TOK, TOK))
    sub, lane = iota((TOK, TOK), 0), iota((TOK, TOK), 1)
    rank_row = jnp.sum(jnp.where(same & (sub < lane), 1.0, 0.0), axis=0, keepdims=True)
    rank_col = jnp.sum(jnp.where(same & (lane < sub), 1.0, 0.0), axis=1, keepdims=True)
    slot_row = picked_row * 8.0 + rank_row
    slot_col = picked_col[:, 0:1] * 8.0 + rank_col
    spread = jnp.where(iota((SLOTS, TOK), 0).astype(F32) == slot_row, 1.0, 0.0).astype(BF16)
    pick = jnp.where(iota((TOK, SLOTS), 1).astype(F32) == slot_col, 1.0, 0.0).astype(BF16)

    for copy in kv[3]:
        copy.wait_recv()

    @pl.when(last)
    def _():
        for copy in relay:
            copy.start()

    pl.semaphore_wait(known.at[0], 2)
    tell(known.at[1], ring(8), e)
    tell(known.at[1], ring(-8), e)

    scores = [None] * 5
    for k in (0, 4, 3, 2, 1):
        if k == 0:
            allowed = (seg_col == seg_row) & (lane <= sub)
        else:
            if k < 4:
                for copy in kv[k - 1]:
                    copy.wait_recv()
            shift = jnp.where(s >= k, 0.0, 1000.0)
            allowed = seg_col == sb[k].astype(F32) + shift
        both = []
        for h in range(2):
            cols = slice(h * HEAD, (h + 1) * HEAD)
            raw = dot_nt(qs[:, cols], kb[k, :, cols]) * HEAD ** (-0.5)
            both.append(jnp.where(allowed, raw, NEGATIVE))
        scores[k] = both
    for h in range(2):
        cols = slice(h * HEAD, (h + 1) * HEAD)
        top = scores[0][h]
        for k in range(1, 5):
            top = jnp.maximum(top, scores[k][h])
        top = jnp.max(top, axis=1, keepdims=True)
        total = jnp.zeros((TOK, TOK), F32)
        numer = jnp.zeros((TOK, HEAD), F32)
        for k in range(5):
            weight = jnp.exp(scores[k][h] - top)
            total = total + weight
            numer = numer + dot(weight.astype(BF16), vb[k, :, cols])
        denom = jnp.sum(total, axis=1, keepdims=True)
        att[c, :, cols] = (numer / denom).astype(BF16)
    att_x = far(att.at[c], att.at[c], pair_s.at[0], pair_r.at[0], s, pe)
    att_x.start()
    for copy in w_loads:
        copy.wait()
    for z in range(4):
        wd[z].wait_recv()
    att_x.wait_recv()

    def reduced(part, sent, came, sends, recvs, emit):
        copies = []

        def go(f, i, to):
            copy = far(sent.at[f, i], came.at[f, i], sends.at[f, i], recvs.at[f, i], s, to)
            copy.start()
            copies.append(copy)
            return copy

        ahead = []
        for f in range(2):
            value = part(lax.rem(zh + 2, 4), f)
            sent[f, 0] = value[:, :QUART].astype(BF16)
            sent[f, 3] = value[:, QUART:].astype(BF16)
            ahead.append((go(f, 0, ue), go(f, 3, de)))
        waits, owns = [], []
        for f in range(2):
            up_value = part(lax.rem(zh + 1, 4), f)
            sent[f, 1] = up_value[:, QUART:].astype(BF16)
            c1 = go(f, 1, ue)
            down_value = part(lax.rem(zh + 3, 4), f)
            sent[f, 4] = down_value[:, :QUART].astype(BF16)
            c4 = go(f, 4, de)
            owns.append(part(zh, f))
            ahead[f][0].wait_recv()
            sent[f, 2] = (up_value[:, :QUART] + came[f, 0].astype(F32)).astype(BF16)
            c2 = go(f, 2, ue)
            ahead[f][1].wait_recv()
            sent[f, 5] = (down_value[:, QUART:] + came[f, 3].astype(F32)).astype(BF16)
            c5 = go(f, 5, de)
            waits.append((c1, c4, c2, c5))
        for f in range(2):
            for copy in waits[f]:
                copy.wait_recv()
            left = owns[f][:, :QUART] + came[f, 2].astype(F32) + came[f, 4].astype(F32)
            right = owns[f][:, QUART:] + came[f, 1].astype(F32) + came[f, 5].astype(F32)
            emit(f, left, right)
        return copies

    def scatter(outs, ins, send, recv):
        @pl.loop(1, NSEQ)
        def _(i):
            to = lax.rem(s + i, NSEQ)
            far(outs.at[to], ins.at[s], send, recv, to, e).start()

        ins[s] = outs[s]

    def arrive(outs, ins, sem):
        pltpu.make_async_copy(outs.at[pl.ds(0, NSEQ - 1)], ins.at[pl.ds(0, NSEQ - 1)], sem).wait()

    def projected(z, f):
        cols = slice(f * HALF, (f + 1) * HALF)
        return dot(att[0], w2[z, 0, :, cols]) + dot(att[1], w2[z, 1, :, cols])

    partial_squares = []

    def to_experts(f, left, right):
        low, high = slice(f * HALF, f * HALF + QUART), slice(f * HALF + QUART, (f + 1) * HALF)
        left = res[:, low].astype(F32) + left
        right = res[:, high].astype(F32) + right
        resid[:, low] = left
        resid[:, high] = right
        partial_squares.append(left * left + right * right)
        gained = (resid[:, f * HALF:(f + 1) * HALF] * gains[:, f * HALF:(f + 1) * HALF]).astype(BF16)
        ob[f] = dot(spread, gained).reshape(NSEQ, 8, HALF).astype(BF16)
        scatter(ob.at[f], rb.at[f], a_s.at[f], a_r.at[f])

    pl.semaphore_wait(known.at[1], 2)
    r1 = reduced(projected, r1s, r1r, r1_s, r1_r, to_experts)

    squares = jnp.sum(partial_squares[0] + partial_squares[1], axis=1, keepdims=True)
    squares = jnp.transpose(jnp.broadcast_to(squares, (TOK, TOK)))[0:8, :]
    ss[0] = squares
    ss_p = far(ss.at[0], sr.at[0], ss_s.at[0], ss_r.at[0], s, pe)
    ss_p.start()

    row, col = iota((ROWS, SLOTS), 0), iota((ROWS, SLOTS), 1)
    tight = jnp.where((row == (col >> 3) * 7 + (col & 7)) & ((col & 7) < 7), 1.0, 0.0).astype(BF16)
    row, col = iota((SLOTS, ROWS), 0), iota((SLOTS, ROWS), 1)
    loose = jnp.where((col == (row >> 3) * 7 + (row & 7)) & ((row & 7) < 7), 1.0, 0.0).astype(BF16)

    first, second = pl.ds(0, ROWS // 2), pl.ds(ROWS // 2, ROWS // 2)
    every = pl.ds(0, ROWS)

    def begin(f):
        def columns(src_e):
            return pl.ds(pl.multiple_of(src_e * COLS + f * HALF, HALF), HALF)

        def pass_on(i, src_e, rows, to):
            part = xb.at[rows, columns(src_e)]
            return far(part, part, ag_s.at[f, i], ag_r.at[f, i], s, to)

        arrive(ob.at[f], rb.at[f], a_r.at[f])
        xb[:, columns(e)] = dot(tight, rb[f].astype(F32).reshape(SLOTS, HALF).astype(BF16)).astype(BF16)
        g = [
            pass_on(0, e, first, ue), pass_on(1, e, second, ue), pass_on(2, e, second, de), pass_on(3, e, first, de),
            pass_on(4, de, first, ue), pass_on(5, ue, second, de),
            pass_on(6, e, every, pe), pass_on(7, de, every, pe), pass_on(8, ue, every, pe), pass_on(9, fe, every, pe),
        ]
        for i in (0, 2, 6, 1, 3):
            g[i].start()
        return g

    def relay_on(g):
        g[0].wait_recv()
        g[4].start()
        g[2].wait_recv()
        g[5].start()

    def share_near(g):
        g[1].wait_recv()
        g[7].start()
        g[3].wait_recv()
        g[8].start()

    def share_far(g):
        g[4].wait_recv()
        g[5].wait_recv()
        g[9].start()

    def absorb(offset, width):
        cols = pl.ds(pl.multiple_of(offset, width), width)
        return dot_nt(xb[:, cols], gu[:, cols])

    gather0 = begin(0)
    ss_p.wait_recv()
    squares = squares + sr[0]
    ss[1] = squares
    ss_z = [far(ss.at[1], sr.at[i], ss_s.at[i], ss_r.at[i], s, to) for i, to in ((1, ue), (2, de), (3, fe))]
    for copy in ss_z:
        copy.start()
    gather1 = begin(1)
    relay_on(gather0)

    for copy in ss_z:
        copy.wait_recv()
    scale_row = lax.rsqrt((squares + sr[1] + sr[2] + sr[3])[0:1, :] / D + EPSILON)
    chosen = jnp.where(iota((NSEQ, TOK), 0).astype(F32) == picked_row, 1.0, 0.0)
    ranked = jnp.where(lane.astype(F32) == rank_col, as_column(scale_row), 0.0)
    osc[...] = exact_dot(chosen, ranked).reshape(NSEQ, 1, TOK)
    scatter(osc, rsc, c_s.at[0], c_r.at[0])

    share_near(gather0)
    for copy in e_loads:
        copy.wait()
    gather0[6].wait_recv()
    gather1[6].wait_recv()
    acc[...] = absorb(zh * 1024, 1024)
    relay_on(gather1)
    share_near(gather1)
    for g in (gather0, gather1):
        g[7].wait_recv()
        g[8].wait_recv()
    acc[...] += absorb((ue // 2) * 1024, 1024)
    share_far(gather0)
    acc[...] += absorb((de // 2) * 1024, 1024)
    gather0[9].wait_recv()
    acc[...] += absorb(fe * COLS, HALF) + absorb(pfe * COLS, HALF)
    share_far(gather1)
    acc[...] += absorb(fe * COLS + HALF, HALF)
    gather1[9].wait_recv()
    acc[...] += absorb(pfe * COLS + HALF, HALF)

    arrive(osc, rsc, c_r.at[0])
    owner = jnp.where(iota((ROWS, NSEQ), 0) // 7 == iota((ROWS, NSEQ), 1), 1.0, 0.0)
    mine = lax.rem(iota((ROWS, TOK), 0), 7) == iota((ROWS, TOK), 1)
    scale = jnp.sum(jnp.where(mine, exact_dot(owner, rsc[...].reshape(NSEQ, TOK)), 0.0), axis=1, keepdims=True)
    gate_sum = acc[:, 0:UNITS] * scale
    up_sum = acc[:, 384:384 + UNITS] * scale
    logit = acc[:, UNITS:UNITS + 1] * scale
    hidden = gate_sum / (1.0 + jnp.exp(-gate_sum)) * up_sum * (1.0 / (1.0 + jnp.exp(-logit)))
    hb[c] = hidden.astype(BF16)
    hid_x = far(hb.at[c], hb.at[c], pair_s.at[1], pair_r.at[1], s, pe)
    hid_x.start()
    for copy in d_loads:
        copy.wait()
    for z in range(4, 8):
        wd[z].wait_recv()
    hid_x.wait_recv()

    def expert_out(z, f):
        cols = slice(f * HALF, (f + 1) * HALF)
        return dot(hb[0], d2[z, 0, :, cols]) + dot(hb[1], d2[z, 1, :, cols])

    def to_tokens(f, left, right):
        yb[f, :, :, :QUART] = dot(loose, left.astype(BF16)).reshape(NSEQ, 8, QUART).astype(BF16)
        yb[f, :, :, QUART:] = dot(loose, right.astype(BF16)).reshape(NSEQ, 8, QUART).astype(BF16)
        scatter(yb.at[f], zb.at[f], b_s.at[f], b_r.at[f])

    r2 = reduced(expert_out, r2s, r2r, r2_s, r2_r, to_tokens)
    for f in range(2):
        cols = slice(f * HALF, (f + 1) * HALF)
        arrive(yb.at[f], zb.at[f], b_r.at[f])
        routed = dot(pick, zb[f].astype(F32).reshape(SLOTS, HALF).astype(BF16))
        out_ref[:, cols] = resid[:, cols] + routed

    for trio in kv:
        for copy in trio:
            copy.wait_send()
    for copy in wd + [att_x, hid_x, *r1, *r2, ss_p, *ss_z, *gather0, *gather1]:
        copy.wait_send()
    for buf, sem in ((ob.at[0], a_s.at[0]), (ob.at[1], a_s.at[1]), (osc, c_s.at[0]), (yb.at[0], b_s.at[0]),
                     (yb.at[1], b_s.at[1])):
        arrive(buf, buf, sem)


def local(
    query_input, key_input, value_input, segment_ids, residual_in, out_weight, norm_gain, router,
    modality, expert_in, gate_weight, up_weight, down_weight,
):
    anywhere = pl.BlockSpec(memory_space=pltpu.HBM)
    vmem = pl.BlockSpec(memory_space=pltpu.VMEM)
    V = pltpu.VMEM
    dma = pltpu.SemaphoreType.DMA
    total = pl.pallas_call(
        kernel,
        out_shape=pltpu.VMEM((TOK, COLS), F32),
        in_specs=[anywhere] * 13,
        out_specs=vmem,
        scratch_shapes=[
            V((TOK, WIDE), BF16),
            V((5, TOK, WIDE), BF16),
            V((5, TOK, WIDE), BF16),
            V((5, 1, TOK), jnp.int32),
            V((1, TOK), jnp.int32),
            V((1, TOK), jnp.int32),
            V((1, COLS), F32),
            V((1, D), BF16),
            V((TOK, COLS), BF16),
            V((4, 2, WIDE, COLS), BF16),
            V((736, D), BF16),
            V((4, 2, UNITS, COLS), BF16),
            V((2, TOK, WIDE), BF16),
            V((2, 6, TOK, QUART), BF16),
            V((2, 6, TOK, QUART), BF16),
            V((2, 8, TOK), F32),
            V((4, 8, TOK), F32),
            V((2, NSEQ, 8, HALF), BF16),
            V((2, NSEQ, 8, HALF), BF16),
            V((NSEQ, 1, TOK), F32),
            V((NSEQ, 1, TOK), F32),
            V((ROWS, D), BF16),
            V((ROWS, 736), F32),
            V((2, ROWS, UNITS), BF16),
            V((2, 6, ROWS, QUART), BF16),
            V((2, 6, ROWS, QUART), BF16),
            V((2, NSEQ, 8, HALF), BF16),
            V((2, NSEQ, 8, HALF), BF16),
            V((TOK, COLS), F32),
            pltpu.SemaphoreType.REGULAR((2,)),
            dma((19,)),
            dma((4, 3)), dma((4, 3)),
            dma((8,)), dma((8,)),
            dma((2,)), dma((2,)),
            dma((2, 6)), dma((2, 6)),
            dma((4,)), dma((4,)),
            dma((2,)), dma((2,)),
            dma((1,)), dma((1,)),
            dma((2, 10)), dma((2, 10)),
            dma((2, 6)), dma((2, 6)),
            dma((2,)), dma((2,)),
        ],
        compiler_params=pltpu.CompilerParams(
            collective_id=0, has_side_effects=True, vmem_limit_bytes=67043328 - 278528),
    )(
        query_input, key_input, value_input, segment_ids.reshape(1, TOK), modality.reshape(1, TOK),
        expert_in.reshape(1, TOK), residual_in, out_weight, norm_gain.reshape(1, COLS),
        router.T, gate_weight[0].T, up_weight[0].T, down_weight[0],
    )
    return total.astype(BF16)


def solution(mesh):
    placed = (
        P("seq", "exp"), P("seq", "exp"), P("seq", "exp"), P("seq"), P("seq", "exp"), P("exp", None), P("exp"),
        P(None, "seq"), P("seq"), P("seq"), P("seq", None, "exp"), P("seq", None, "exp"), P("seq", "exp", None),
    )
    return jax.shard_map(local, mesh=mesh, in_specs=placed, out_specs=P("seq", "exp"), check_vma=False)
```

time: 89 us -> 86.1 us (0.967)
  Pallas kernels: 88.3 us -> 85.3 us
    pallas_call x1, Pallas kernels: 88.3 us -> 85.3 us  [local(): pl.pallas_call(kernel, out_shape=pltpu.VMEM((TOK, COLS), F32), in_specs=[...]
where the time goes in v3:
time: 86.1 us; the launch traced here: 86 us
  Pallas kernels  85.3 us (99%)
    pallas_call x1, Pallas kernels, local(): pl.pallas_call(kernel, out_shape=pltpu.VMEM((TOK, COLS), F32), in_specs=[...  85.3 us

profile of v3, /device:TPU:1, one launch (start us, length us, event | category | flops | bytes accessed | tf_op | source)
XLA Modules:
  0.0 86.0 jit_solution(8843299064712586960)
XLA Ops:
  0.0 85.3 %shard_map.127 = f32[128,512]{1,0:T(8,128)S(1)} custom-call(bf16[128,256]{1,0:T(8,128)(2,1)} %q_hbm.1, bf16[128,256]{1,0:T(8,128)(2,1)} %k_hbm.1, bf16[128,256]{1,0:T(8,128)(2,1)} %v_hbm.1, s32[1,128]{1,0:T(1,128)} %bitcast.17, s32[1,128]{1,0:T(1,128)} %bitcast.18, s32[1,128]{1,0:T(1,128)} %bitcast.19, bf16[128,512]{1,0:T(8,128)(2,1)} %res_hbm.1, ...), custom_call_target="tpu_custom_call" | custom-call | tf_op jit(solution)/shard_map/pallas_call | solution.py:428
  85.3 0.7 convert_element_type.3

commit v4 on v3

--- a/solution.py
+++ b/solution.py
@@ -335,15 +335,13 @@
         cols = pl.ds(pl.multiple_of(offset, width), width)
         return dot_nt(xb[:, cols], gu[:, cols])
 
-    gather0 = begin(0)
     ss_p.wait_recv()
     squares = squares + sr[0]
     ss[1] = squares
-    ss_z = [far(ss.at[1], sr.at[i], ss_s.at[i], ss_r.at[i], s, to) for i, to in ((1, ue), (2, de), (3, fe))]
+    ss_z = [far(ss.at[1], sr.at[i], ss_s.at[i], ss_r.at[i], s, to) for i, to in ((3, fe), (1, ue), (2, de))]
     for copy in ss_z:
         copy.start()
-    gather1 = begin(1)
-    relay_on(gather0)
+    gather0 = begin(0)
 
     for copy in ss_z:
         copy.wait_recv()
@@ -353,6 +351,8 @@
     osc[...] = exact_dot(chosen, ranked).reshape(NSEQ, 1, TOK)
     scatter(osc, rsc, c_s.at[0], c_r.at[0])
 
+    gather1 = begin(1)
+    relay_on(gather0)
     share_near(gather0)
     for copy in e_loads:
         copy.wait()

time: 86.1 us -> 84.3 us (0.979)
  Pallas kernels: 85.3 us -> 83.2 us
    pallas_call x1, Pallas kernels: 85.3 us -> 83.2 us  [local(): pl.pallas_call(kernel, out_shape=pltpu.VMEM((TOK, COLS), F32), in_specs=[...]
where the time goes in v4:
time: 84.3 us; the launch traced here: 83.9 us
  Pallas kernels  83.2 us (99%)
    pallas_call x1, Pallas kernels, local(): pl.pallas_call(kernel, out_shape=pltpu.VMEM((TOK, COLS), F32), in_specs=[...  83.2 us

profile of v4, /device:TPU:1, one launch (start us, length us, event | category | flops | bytes accessed | tf_op | source)
XLA Modules:
  0.0 83.9 jit_solution(11467326515741413117)
XLA Ops:
  0.0 83.2 %shard_map.127 = f32[128,512]{1,0:T(8,128)S(1)} custom-call(bf16[128,256]{1,0:T(8,128)(2,1)} %q_hbm.1, bf16[128,256]{1,0:T(8,128)(2,1)} %k_hbm.1, bf16[128,256]{1,0:T(8,128)(2,1)} %v_hbm.1, s32[1,128]{1,0:T(1,128)} %bitcast.17, s32[1,128]{1,0:T(1,128)} %bitcast.18, s32[1,128]{1,0:T(1,128)} %bitcast.19, bf16[128,512]{1,0:T(8,128)(2,1)} %res_hbm.1, ...), custom_call_target="tpu_custom_call" | custom-call | tf_op jit(solution)/shard_map/pallas_call | solution.py:428
  83.2 0.7 convert_element_type.3

commit v5 on v4

--- a/solution.py
+++ b/solution.py
@@ -253,7 +253,7 @@
     def scatter(outs, ins, send, recv):
         @pl.loop(1, NSEQ)
         def _(i):
-            to = lax.rem(s + i, NSEQ)
+            to = lax.rem(s + lax.rem(i + 11, NSEQ - 1) + 1, NSEQ)
             far(outs.at[to], ins.at[s], send, recv, to, e).start()
 
         ins[s] = outs[s]

time: 84.3 us -> 84.9 us (level)
  Pallas kernels: 83.2 us -> 84.1 us
    pallas_call x1, Pallas kernels: 83.2 us -> 84.1 us  [local(): pl.pallas_call(kernel, out_shape=pltpu.VMEM((TOK, COLS), F32), in_specs=[...]
where the time goes in v5:
time: 84.9 us; the launch traced here: 84.8 us
  Pallas kernels  84.1 us (99%)
    pallas_call x1, Pallas kernels, local(): pl.pallas_call(kernel, out_shape=pltpu.VMEM((TOK, COLS), F32), in_specs=[...  84.1 us

profile of v5, /device:TPU:1, one launch (start us, length us, event | category | flops | bytes accessed | tf_op | source)
XLA Modules:
  0.0 84.8 jit_solution(272791372962864527)
XLA Ops:
  0.0 84.1 %shard_map.127 = f32[128,512]{1,0:T(8,128)S(1)} custom-call(bf16[128,256]{1,0:T(8,128)(2,1)} %q_hbm.1, bf16[128,256]{1,0:T(8,128)(2,1)} %k_hbm.1, bf16[128,256]{1,0:T(8,128)(2,1)} %v_hbm.1, s32[1,128]{1,0:T(1,128)} %bitcast.17, s32[1,128]{1,0:T(1,128)} %bitcast.18, s32[1,128]{1,0:T(1,128)} %bitcast.19, bf16[128,512]{1,0:T(8,128)(2,1)} %res_hbm.1, ...), custom_call_target="tpu_custom_call" | custom-call | tf_op jit(solution)/shard_map/pallas_call | solution.py:428
  84.1 0.7 convert_element_type.3
